TPU v7x, 32 devices: a 4x4x1 block of a 4x4x8 slice. The times are simulated.
32 devices in a mesh: dp: 1 (over z), cp: 4 (over y), tp: 8 (over x, core).
Axes of the slice: x: 4, y: 4, z: 1, core: 2. Of those that a mesh axis runs over, the one named last changes fastest.
The devices are a block of a 4x4x8 slice.
Arguments:
- hidden_in: bfloat16 [6144, 2048], P(('dp', 'cp', 'tp'))
- w_query: bfloat16 [2048, 16, 128], P(None, 'tp')
- w_key: bfloat16 [2048, 16, 128], P(None, 'tp')
- w_value: bfloat16 [2048, 16, 128], P(None, 'tp')
- w_out: bfloat16 [16, 128, 2048], P('tp')
- expert_idx: int32 [6144, 6], P(('dp', 'cp', 'tp'))
- gate_vals: float32 [6144, 6], P(('dp', 'cp', 'tp'))
- w_gate: bfloat16 [64, 2048, 1408], P(('cp', 'tp'))
- w_up: bfloat16 [64, 2048, 1408], P(('cp', 'tp'))
- w_down: bfloat16 [64, 1408, 2048], P(('cp', 'tp'))
Outputs:
- output: bfloat16 [6144, 2048], P(('dp', 'cp', 'tp'))
All inputs are finite; a program needn't handle non-finite values.
Results may differ from a plain program's by a relative error of at most 0.014792.
Values are sent between devices in bfloat16 or wider.
A program may use at most 768 MiB of HBM per device.

v0:
```python
import math
import jax
import jax.numpy as jnp
from jax import lax
from jax.sharding import PartitionSpec as P


def row_positions(row_ids, block_rows, cp_devs):
    chunk_rows = block_rows // 2
    block_id = row_ids // block_rows
    offset_in = row_ids % block_rows
    return jnp.where(offset_in < chunk_rows, block_id * chunk_rows + offset_in, (2 * cp_devs - 1 - block_id) * chunk_rows + offset_in - chunk_rows)


def attend_blocks(query_vecs, key_all, value_all, q_position, k_position):
    row_count, kv_heads, group_size, head_dim = query_vecs.shape
    q_block = math.gcd(row_count, 128)
    n_blocks = row_count // q_block
    score_scale = head_dim ** -0.5

    def one_block(operands):
        q_blk, q_place = operands
        scores = jnp.einsum('qgrd,kgd->qgrk', q_blk, key_all, preferred_element_type=jnp.float32) * score_scale
        allowed = k_position[None, None, None, :] <= q_place[:, None, None, None]
        scores = jnp.where(allowed, scores, -1e30)
        attn_prob = jax.nn.softmax(scores, axis=-1).astype(jnp.bfloat16)
        attn_out = jnp.einsum('qgrk,kgd->qgrd', attn_prob, value_all, preferred_element_type=jnp.float32)
        return attn_out.astype(jnp.bfloat16)

    blocks = lax.map(one_block, (query_vecs.reshape(n_blocks, q_block, kv_heads, group_size, head_dim), q_position.reshape(n_blocks, q_block)))
    return blocks.reshape(row_count, kv_heads * group_size * head_dim)


def attention_residual(hidden_in, w_query, w_key, w_value, w_out, cp_devs):
    hidden = hidden_in.shape[1]
    kv_heads = w_key.shape[1]
    head_dim = w_key.shape[2]
    group_size = w_query.shape[1] // kv_heads
    gathered = lax.all_gather(hidden_in, 'tp', axis=0, tiled=True)
    block_rows = gathered.shape[0]
    query_vecs = jnp.dot(gathered, w_query.reshape(hidden, -1), preferred_element_type=jnp.float32).astype(jnp.bfloat16).reshape(block_rows, kv_heads, group_size, head_dim)
    key_loc = jnp.dot(gathered, w_key.reshape(hidden, -1), preferred_element_type=jnp.float32).astype(jnp.bfloat16)
    value_loc = jnp.dot(gathered, w_value.reshape(hidden, -1), preferred_element_type=jnp.float32).astype(jnp.bfloat16)
    key_all = lax.all_gather(key_loc, 'cp', axis=0, tiled=True).reshape(-1, kv_heads, head_dim)
    value_all = lax.all_gather(value_loc, 'cp', axis=0, tiled=True).reshape(-1, kv_heads, head_dim)
    cp_rank = lax.axis_index('cp')
    q_position = row_positions(cp_rank * block_rows + jnp.arange(block_rows), block_rows, cp_devs)
    k_position = row_positions(jnp.arange(block_rows * cp_devs), block_rows, cp_devs)
    attn_all = attend_blocks(query_vecs, key_all, value_all, q_position, k_position)
    part_sum = jnp.dot(attn_all, w_out.reshape(-1, hidden), preferred_element_type=jnp.float32)
    reduced = lax.psum_scatter(part_sum, 'tp', scatter_dimension=0, tiled=True)
    return (hidden_in.astype(jnp.float32) + reduced).astype(jnp.bfloat16)


def solution(mesh):
    cp_devs = mesh.shape['cp']
    group_devs = cp_devs * mesh.shape['tp']
    row_spec = P(('dp', 'cp', 'tp'), None)
    head_spec = P(None, 'tp', None)
    expert_spec = P(('cp', 'tp'), None, None)

    def device_step(hidden_in, w_query, w_key, w_value, w_out, expert_idx, gate_vals, w_gate, w_up, w_down):
        tok_dev, hidden = hidden_in.shape
        top_k = expert_idx.shape[1]
        local_exp = w_gate.shape[0]
        experts = local_exp * group_devs
        capacity = tok_dev * top_k // experts
        resid_h = attention_residual(hidden_in, w_query, w_key, w_value, w_out, cp_devs)
        flat_idx = expert_idx.reshape(-1)
        hit_mask = flat_idx[:, None] == jnp.arange(experts)[None, :]
        slot_all = jnp.cumsum(hit_mask.astype(jnp.int32), axis=0) - 1
        slot_ids = jnp.sum(jnp.where(hit_mask, slot_all, 0), axis=1)
        dest_row = flat_idx * capacity + slot_ids
        src_rows = jnp.zeros((experts * capacity,), jnp.int32).at[dest_row].set(jnp.arange(tok_dev * top_k, dtype=jnp.int32) // top_k)
        send_buf = jnp.take(resid_h, src_rows, axis=0)
        recv_buf = lax.all_to_all(send_buf, ('cp', 'tp'), 0, 0, tiled=True)
        expert_in = recv_buf.reshape(group_devs, local_exp, capacity, hidden)
        gate_act = jnp.einsum('gech,ehf->gecf', expert_in, w_gate, preferred_element_type=jnp.float32)
        up_act = jnp.einsum('gech,ehf->gecf', expert_in, w_up, preferred_element_type=jnp.float32)
        hidden_act = (jax.nn.silu(gate_act) * up_act).astype(jnp.bfloat16)
        expert_out = jnp.einsum('gecf,efh->gech', hidden_act, w_down, preferred_element_type=jnp.float32).astype(jnp.bfloat16)
        returned = lax.all_to_all(expert_out.reshape(experts * capacity, hidden), ('cp', 'tp'), 0, 0, tiled=True)
        per_choice = jnp.take(returned, dest_row, axis=0).reshape(tok_dev, top_k, hidden)
        moe_sum = jnp.sum(gate_vals[:, :, None] * per_choice, axis=1)
        return (resid_h.astype(jnp.float32) + moe_sum).astype(jnp.bfloat16)

    return jax.shard_map(device_step, mesh=mesh, in_specs=(row_spec, head_spec, head_spec, head_spec, P('tp', None, None), row_spec, row_spec, expert_spec, expert_spec, expert_spec), out_specs=row_spec, check_vma=False)
```

profile of v0, /device:TPU:97, one launch (start us, length us, event | category | flops | bytes accessed | tf_op | source)
XLA Modules:
  0.0 549.8 jit_solution(2781580902292079235)
XLA Ops:
  7.4 43.9 %all-gather.4.cloned.1.call-done = bf16[1536,2048]{1,0:T(8,128)(2,1)} async-done(((bf16[192,2048]{1,0:T(8,128)(2,1)}), bf16[1536,2048]{1,0:T(8,128)(2,1)}) %all-gather.4.cloned.1.call-update) | async-done | bytes 6291472 | tf_op jit(solution)/shard_map/all_gather | solution.py:39
  51.3 5.8 %convolution_convert_fusion.1 = bf16[1536,256]{1,0:T(8,128)(2,1)} fusion(bf16[1536,2048]{1,0:T(8,128)(2,1)} %all-gather.4.cloned.1.call-done, bf16[256,8,2,128]{3,2,1,0:T(2,128)(2,1)} %bitcast.145), kind=kOutput, calls=%fused_computation.55 | convolution fusion | flops 1611005952 | bytes 8126464 | tf_op jit(solution)/shard_map/dot_general | solution.py:42
  57.3 5.5 %convolution_convert_fusion = bf16[1536,256]{1,0:T(8,128)(2,1)} fusion(bf16[1536,2048]{1,0:T(8,128)(2,1)} %all-gather.4.cloned.1.call-done, bf16[256,8,2,128]{3,2,1,0:T(2,128)(2,1)S(1)} %bitcast.146), kind=kOutput, calls=%fused_computation.54 | convolution fusion | flops 1611005952 | bytes 8126464 | tf_op jit(solution)/shard_map/dot_general | solution.py:43
  63.2 4.8 convolution_convert_fusion.2
  68.2 25.4 %all-gather.6.cloned.1.call-done = bf16[6144,256]{1,0:T(8,128)(2,1)} async-done(((bf16[1536,256]{1,0:T(8,128)(2,1)}), bf16[6144,256]{1,0:T(8,128)(2,1)}) %all-gather.6.cloned.1.call-update) | async-done | bytes 3145744 | tf_op jit(solution)/shard_map/all_gather | solution.py:44
  93.6 4.1 copy_bitcast_fusion.3
  97.7 34.5 %all-gather.8.cloned.1.call-done = bf16[6144,256]{1,0:T(8,128)(2,1)} async-done(((bf16[1536,256]{1,0:T(8,128)(2,1)}), bf16[6144,256]{1,0:T(8,128)(2,1)}) %all-gather.8.cloned.1.call-update) | async-done | bytes 3145744 | tf_op jit(solution)/shard_map/all_gather | solution.py:45
  132.2 4.1 copy_bitcast_fusion.2
  136.3 92.4 %while.11 = (s32[]{:T(128)}, bf16[12,128,2,1,128]{4,2,1,0,3:T(2,128)(2,1)S(1)}, s32[12,128]{1,0:T(8,128)S(1)}, bf16[12,128,2,1,128]{4,2,1,0,3:T(2,128)(2,1)S(1)}...) while((s32[]{:T(128)}, ...), condition=%wide.region_3.4_spmd.clone, body=%wide.region_0.3_spmd.clone.sunk | while | flops 818830848 | bytes 39770748 | solution.py:30
  136.9 3.6 fusion.90
  140.4 1.0 fusion.91
  142.3 1.5 fusion.92
  144.6 3.6 fusion.90
  148.1 1.0 fusion.91
  150.0 1.5 fusion.92
  152.3 3.6 fusion.90
  155.8 1.0 fusion.91
  157.7 1.5 fusion.92
  160.0 3.6 fusion.90
  163.5 1.0 fusion.91
  165.4 1.5 fusion.92
  167.7 3.6 fusion.90
  171.3 1.0 fusion.91
  173.1 1.5 fusion.92
  175.4 3.6 fusion.90
  179.0 1.0 fusion.91
  180.8 1.5 fusion.92
  183.1 3.6 fusion.90
  186.7 1.0 fusion.91
  188.6 1.5 fusion.92
  190.8 3.6 fusion.90
  194.4 1.0 fusion.91
  196.3 1.5 fusion.92
  198.5 3.6 fusion.90
  202.1 1.0 fusion.91
  204.0 1.5 fusion.92
  206.2 3.6 fusion.90
  209.8 1.0 fusion.91
  211.7 1.5 fusion.92
  213.9 3.6 fusion.90
  219.4 1.5 fusion.92
  221.6 3.6 fusion.90
  227.1 1.5 fusion.92
  228.7 6.4 %fusion.47 = f32[1536,2048]{1,0:T(8,128)} fusion(bf16[256,2048]{1,0:T(8,128)(2,1)S(1)} %bitcast.135, bf16[192,8,2,128]{3,2,1,0:T(2,128)(2,1)S(1)} %bitcast.140), kind=kOutput, calls=%fused_computation.65 | convolution fusion | flops 1610612736 | bytes 14417920 | tf_op jit(solution)/shard_map/dot_general | solution.py:50
  236.5 18.1 %reduce-window.6 = s32[64,9,128]{2,1,0:T(8,128)S(1)} reduce-window(s32[64,9,128]{2,1,0:T(8,128)S(1)} %fusion.50, s32[]{:T(128)} %constant.102.clone.1), window={size=1x1x128 pad=0_0x0_0x127_0}, to_apply=%region_5.6 | reduce-window | flops 9363456 | bytes 589828 | tf_op jit(solution)/shard_map/reduce-window
  255.6 6.7 %scatter_custom_fusion = s32[1152]{0:T(1024)S(1)} fusion(s32[1152]{0:T(1024)S(1)} %fusion.62, s32[1152]{0:T(1024)S(1)} %add_select_fusion.1, s32[]{:T(128)} %constant.102.clone.1), kind=kCustom, calls=%fused_computation.101 | custom fusion | bytes 4612 | tf_op jit(solution)/shard_map/scatter | solution.py:74
  262.5 42.8 %reduce-scatter.2.cloned.1.call-done = f32[192,2048]{1,0:T(8,128)} async-done(((f32[1536,2048]{1,0:T(8,128)}), f32[192,2048]{1,0:T(8,128)}) %reduce-scatter.2.cloned.1.call-update) | async-done | bytes 1572880 | tf_op jit(solution)/shard_map/reduce_scatter | solution.py:51
  305.2 1.6 add_convert_fusion.1
  306.8 5.9 %gather_fusion = bf16[1152,2048]{1,0:T(8,128)(2,1)} fusion(bf16[192,2048]{1,0:T(8,128)(2,1)S(1)} %add_convert_fusion.1, s32[2048]{0:T(1024)S(1)} %pad_clamp_fusion.1), kind=kCustom, calls=%fused_computation | custom fusion | bytes 9441792 | tf_op jit(solution)/shard_map/jit(_take)/gather | solution.py:75
  312.8 7.2 %gather.13 = bf16[32,36,2048]{2,1,0:T(8,128)(2,1)} reshape(bf16[1152,2048]{1,0:T(8,128)(2,1)} %gather_fusion) | data formatting | bytes 9437184 | tf_op jit(solution)/shard_map/jit(_take)/gather | solution.py:75
  320.0 3.0 broadcast_select_fusion
  323.0 71.1 %all_to_all.18 = bf16[32,36,2048]{2,1,0:T(8,128)(2,1)S(1)} all-to-all(bf16[32,36,2048]{2,1,0:T(8,128)(2,1)S(1)} %broadcast_select_fusion), channel_id=1, replica_groups=mesh['dp'=1,'cp'=4,'tp'=8] {'cp','tp'}, dimensions={0} | all-to-all | bytes 9437184 | tf_op jit(solution)/shard_map/all_to_all | solution.py:76
  394.1 2.6 copy.42
  396.7 12.2 %fusion.28 = f32[2,32,18,1408]{3,1,2,0:T(8,128)} fusion(bf16[32,2,18,2048]{3,0,2,1:T(8,128)(2,1)S(1)} %bitcast.136, bf16[2,2048,1408]{2,1,0:T(8,128)(2,1)} %param.20), kind=kOutput, calls=%fused_computation.39 | convolution fusion | flops 6643777536 | bytes 22740992 | tf_op jit(solution)/shard_map/gech,ehf->gecf/dot_general | solution.py:79
  408.9 10.2 %fusion.32 = bf16[32,2,18,1408]{3,0,2,1:T(8,128)(2,1)S(1)} fusion(f32[2,32,18,1408]{3,1,2,0:T(8,128)} %fusion.28, bf16[32,2,18,2048]{3,0,2,1:T(8,128)(2,1)S(1)} %bitcast.137, bf16[2,2048,1408]{2,1,0:T(8,128)(2,1)S(1)} %bitcast.144), kind=kOutput, calls=%fused_computation.44 | convolution fusion | flops 6653509632 | bytes 25985024 | tf_op jit(solution)/shard_map/gech,ehf->gecf/dot_general | solution.py:78
  419.2 10.8 %fusion.38 = bf16[2,32,18,2048]{3,1,2,0:T(8,128)(2,1)S(1)} fusion(bf16[32,2,18,1408]{3,0,2,1:T(8,128)(2,1)S(1)} %fusion.32, bf16[2,1408,2048]{2,1,0:T(8,128)(2,1)} %param.21), kind=kOutput, calls=%fused_computation.51 | convolution fusion | flops 6646136832 | bytes 19496960 | tf_op jit(solution)/shard_map/gecf,efh->gech/dot_general | solution.py:81
  429.9 4.9 copy.43
  434.9 4.9 all-to-all-start.1
  440.4 63.8 %all-to-all-done.1 = bf16[32,36,2048]{2,1,0:T(8,128)(2,1)} async-done(((bf16[32,36,2048]{2,1,0:T(8,128)(2,1)}), bf16[32,36,2048]{2,1,0:T(8,128)(2,1)}, u32[]{:S(2)}, u32[]{:S(2)}) %all-to-all-start.1) | async-done | bytes 4718624 | tf_op jit(solution)/shard_map/all_to_all | solution.py:82
  504.2 7.2 %all_to_all.15 = bf16[1152,2048]{1,0:T(8,128)(2,1)} reshape(bf16[32,36,2048]{2,1,0:T(8,128)(2,1)} %all-to-all-done.1) | data formatting | bytes 9437184 | tf_op jit(solution)/shard_map/all_to_all | solution.py:82
  511.4 13.6 %gather_fusion.1 = bf16[1152,2048]{1,0:T(8,128)(2,1)} fusion(bf16[1152,2048]{1,0:T(8,128)(2,1)} %all_to_all.15, s32[2048]{0:T(1024)S(1)} %pad_clamp_fusion), kind=kCustom, calls=%fused_computation.1 | custom fusion | bytes 9441792 | tf_op jit(solution)/shard_map/jit(_take)/gather | solution.py:83
  525.0 8.5 %gather.15 = bf16[192,6,2048]{2,1,0:T(8,128)(2,1)} reshape(bf16[1152,2048]{1,0:T(8,128)(2,1)} %gather_fusion.1) | data formatting | bytes 9437184 | tf_op jit(solution)/shard_map/jit(_take)/gather | solution.py:83
  533.5 8.2 %multiply_reduce_fusion = f32[192,2048]{1,0:T(8,128)S(1)} fusion(bf16[192,6,2048]{2,1,0:T(8,128)(2,1)} %gather.15, f32[192,6]{1,0:T(8,128)S(1)} %copy.34, pred[192,6]{1,0:T(8,128)(4,1)S(1)} %copy.40), kind=kLoop, calls=%fused_computation.36 | loop fusion | flops 9043968 | bytes 6297216 | tf_op jit(solution)/shard_map/reduce_sum | solution.py:84
  541.7 1.1 add_convert_fusion
  (141 shorter events, 25.1 us)
Async XLA Ops:
  6.5 222.2 %copy-start = (bf16[2,128,2048]{2,1,0:T(8,128)(2,1)S(1)}, bf16[2,128,2048]{2,1,0:T(8,128)(2,1)}, u32[]{:S(2)}) copy-start(bf16[2,128,2048]{2,1,0:T(8,128)(2,1)} %param.16) | copy-start | bytes 3145732
  6.6 44.8 %all-gather.4.cloned.1.call-start = ((), (), s32[]{:S(2)}) async-start(), calls=%async_computation.3 | async-start | bytes 7077888 | tf_op jit(solution)/shard_map/all_gather | solution.py:39
  7.3 86.3 %all-gather.6.cloned.1.call-start = ((), (), s32[]{:S(2)}) async-start(), calls=%async_computation.4 | async-start | bytes 3932160 | tf_op jit(solution)/shard_map/all_gather | solution.py:44
  51.3 6.0 %copy-start.6 = (bf16[2048,2,128]{2,1,0:T(2,128)(2,1)S(1)}, bf16[2048,2,128]{2,1,0:T(2,128)(2,1)}, u32[]{:S(2)}) copy-start(bf16[2048,2,128]{2,1,0:T(2,128)(2,1)} %param.15) | copy-start | bytes 3145732
  57.2 75.0 %all-gather.8.cloned.1.call-start = ((), (), s32[]{:S(2)}) async-start(), calls=%async_computation.5 | async-start | bytes 3932160 | tf_op jit(solution)/shard_map/all_gather | solution.py:45
  62.9 242.4 %reduce-scatter.2.cloned.1.call-start = ((), (), s32[]{:S(2)}) async-start(), calls=%async_computation.6 | async-start | bytes 14155776 | tf_op jit(solution)/shard_map/reduce_scatter | solution.py:51
  140.4 1.9 copy-start.2
  148.1 1.9 copy-start.2
  155.8 1.9 copy-start.2
  163.5 1.9 copy-start.2
  171.2 1.9 copy-start.2
  178.9 1.9 copy-start.2
  186.7 1.9 copy-start.2
  194.4 1.9 copy-start.2
  202.1 1.9 copy-start.2
  209.8 1.9 copy-start.2
  217.5 1.9 copy-start.2
  225.2 1.9 copy-start.2
  235.1 0.7 copy-start.4
  235.8 69.5 %copy-start.3 = (bf16[192,2048]{1,0:T(8,128)(2,1)S(1)}, bf16[192,2048]{1,0:T(8,128)(2,1)}, u32[]{:S(2)}) copy-start(bf16[192,2048]{1,0:T(8,128)(2,1)} %param.12) | copy-start | bytes 2359300
  394.1 14.8 %slice-start = ((s8[11534336]{0:T(1024)(128)(4,1)}), s8[3145728]{0:T(1024)(128)(4,1)S(1)}, s32[]{:S(2)}) async-start(s8[11534336]{0:T(1024)(128)(4,1)} %bitcast.143), calls=%async_computation.7 | async-start | bytes 6291456
  396.7 12.2 %slice-start.1 = ((s8[11534336]{0:T(1024)(128)(4,1)}), s8[4194304]{0:T(1024)(128)(4,1)S(1)}, s32[]{:S(2)}) async-start(s8[11534336]{0:T(1024)(128)(4,1)} %bitcast.143), calls=%async_computation.8 | async-start | bytes 8388608
  396.7 12.2 %slice-start.2 = ((s8[11534336]{0:T(1024)(128)(4,1)}), s8[4194304]{0:T(1024)(128)(4,1)S(1)}, s32[]{:S(2)}) async-start(s8[11534336]{0:T(1024)(128)(4,1)} %bitcast.143), calls=%async_computation.9 | async-start | bytes 8388608
  434.9 5.1 copy-start.5
  434.9 69.3 %all-to-all-start.1 = ((bf16[32,36,2048]{2,1,0:T(8,128)(2,1)}), bf16[32,36,2048]{2,1,0:T(8,128)(2,1)}, u32[]{:S(2)}, u32[]{:S(2)}) async-start(bf16[32,36,2048]{2,1,0:T(8,128)(2,1)} %copy.43), calls=%async_computation.2 | async-start | bytes 10485760 | tf_op jit(solution)/shard_map/all_to_all | solution.py:82
  524.9 17.8 %copy-start.1 = (bf16[2,128,2048]{2,1,0:T(8,128)(2,1)S(1)}, bf16[2,128,2048]{2,1,0:T(8,128)(2,1)}, u32[]{:S(2)}) copy-start(bf16[2,128,2048]{2,1,0:T(8,128)(2,1)} %param.16) | copy-start | bytes 3145732
Sparse Core Ops, SparseCore 0:
  8.9 42.3 all-gather.3
  57.3 36.2 all-gather.5
  95.2 36.9 all-gather.7
  235.3 69.9 reduce-scatter.1
where the time goes:
time: 559 us; the launch traced here: 550 us
  waiting for transfers between devices  211 us (38%)
  matrix products  117 us (21%)
  local copies, waits for them, and re-layouts  79.9 us (14%)
  blocking collectives  71.1 us (13%)
  other arithmetic  50.9 us (9%)
  between operations  13.9 us (2%)
    all_to_all x1, blocking collectives, device_step(): recv_buf = lax.all_to_all(send_buf, ('cp', 'tp'), 0, 0, tiled=True)  71.1 us
    all_to_all x1, waiting for transfers between devices, device_step(): lax.all_to_all(expert_out.reshape(experts * capacity, hidden), ('cp', 'tp...  63.8 us
    all_gather x1, waiting for transfers between devices, attention_residual(): gathered = lax.all_gather(hidden_in, 'tp', axis=0, tiled=True)  43.9 us
    reduce_scatter x1, waiting for transfers between devices, attention_residual(): reduced = lax.psum_scatter(part_sum, 'tp', scatter_dimension=0, tiled=True)  42.8 us
    dot_general x12, matrix products, one_block(): jnp.einsum('qgrd,kgd->qgrk', q_blk, key_all, preferred_element_type=jnp.f...  42.7 us
    all_gather x1, waiting for transfers between devices, attention_residual(): lax.all_gather(value_loc, 'cp', axis=0, tiled=True)  34.5 us
    all_gather x1, waiting for transfers between devices, attention_residual(): lax.all_gather(key_loc, 'cp', axis=0, tiled=True)  25.4 us
    gather x2, local copies, waits for them, and re-layouts, device_step(): jnp.take(returned, dest_row, axis=0).reshape(tok_dev, top_k, hidden)  22.1 us
  transfers between devices with their start and end apart: 5, of which 5 were waited for; matrix products, arithmetic and copies ran while one was open for 8% of the time, Pallas kernels for 0%

commit v1 on v0

v1 whole, which is shorter than its diff:
```python
import functools
import math
import jax
import jax.numpy as jnp
from jax import lax
from jax.experimental import pallas as pl
from jax.experimental.pallas import tpu as pltpu

LANES = 128
VMEM_BYTES = 66 * 1024 * 1024


CORES = 2


def spread_order(cp_devs, tp_devs):
    x_devs = tp_devs // CORES
    row, col = lax.axis_index('cp'), lax.axis_index('tp') // CORES
    core = lax.rem(lax.axis_index('tp'), CORES)
    hops = lambda d, n: min(d, n - d)
    chips = [(dx, dy) for dx in range(x_devs) for dy in range(cp_devs)]
    chips.sort(key=lambda o: (-(hops(o[0], x_devs) + hops(o[1], cp_devs)), abs(hops(o[0], x_devs) - hops(o[1], cp_devs)), (o[0] * 3 + o[1] * 5) % 4))
    for dc in range(CORES):
        for dx, dy in chips:
            if dx or dy or dc:
                yield lax.rem(row + dy, cp_devs) * tp_devs + lax.rem(col + dx, x_devs) * CORES + lax.rem(core + dc, CORES)


def moe_kernel(cp_devs, tp_devs, chunks, src_ref, pos_ref, gate_ref, h_ref, wg_ref, wu_ref, wd_ref, y_ref,
               send, recv, xbuf, wgu, wdv, act, wide, zsend, ret, w_sem, loc_sem, dsend_sem, drecv_sem, rsend_sem, rrecv_sem):
    n_dev = cp_devs * tp_devs
    local_exp = wg_ref.shape[0]
    tok_dev, sub = h_ref.shape[0], h_ref.shape[1]
    slots = send.shape[2]
    rows = n_dev * slots
    gu_tiles, dn_tiles = wgu.shape[1], wdv.shape[1]
    dn_cols = wdv.shape[3]
    top_k = gate_ref.shape[0] // tok_dev
    me = lax.axis_index('cp') * tp_devs + lax.axis_index('tp')

    def place(dev):
        return {'cp': dev // tp_devs, 'tp': lax.rem(dev, tp_devs)}

    barrier = pltpu.get_barrier_semaphore()

    def greet(p, carry):
        pl.semaphore_signal(barrier, inc=1, device_id=place(lax.rem(me + p, n_dev)), device_id_type=pl.DeviceIdType.MESH)
        return carry

    lax.fori_loop(1, n_dev, greet, 0)

    def gu_copy(e, j, half, ref):
        return pltpu.make_async_copy(ref.at[e, :, pl.ds(pl.multiple_of(j * LANES, LANES), LANES)],
                                     wgu.at[e, j, :, pl.ds(half * LANES, LANES)], w_sem.at[0, e])

    def dn_copy(e, j):
        return pltpu.make_async_copy(wd_ref.at[e, :, pl.ds(pl.multiple_of(j * dn_cols, dn_cols), dn_cols)], wdv.at[e, j], w_sem.at[1, e])

    for e in range(local_exp):
        @pl.loop(0, gu_tiles)
        def _(j):
            gu_copy(e, j, 0, wg_ref).start()
            gu_copy(e, j, 1, wu_ref).start()

        @pl.loop(0, dn_tiles)
        def _(j):
            dn_copy(e, j).start()

    def fill(dev, carry):
        for c in range(chunks):
            for s in range(slots):
                send[c, dev, s] = h_ref[src_ref[(c * n_dev + dev) * slots + s]]
        return carry

    lax.fori_loop(0, n_dev, fill, 0)
    pl.semaphore_wait(barrier, n_dev - 1)

    def dispatch(c, dev):
        return pltpu.make_async_remote_copy(src_ref=send.at[c, dev], dst_ref=recv.at[c, me], send_sem=dsend_sem.at[c], recv_sem=drecv_sem.at[c],
                                            device_id=place(dev), device_id_type=pl.DeviceIdType.MESH)

    def give_back(c, dev):
        return pltpu.make_async_remote_copy(src_ref=zsend.at[c, dev], dst_ref=ret.at[c, me], send_sem=rsend_sem.at[c], recv_sem=rrecv_sem.at[c],
                                            device_id=place(dev), device_id_type=pl.DeviceIdType.MESH)

    def all_of(copy, c, what):
        if what == 'start':
            for dev in spread_order(cp_devs, tp_devs):
                copy(c, dev).start()
            return
        far = pl.ds(0, n_dev - 1)
        if copy is dispatch:
            every = pltpu.make_async_remote_copy(src_ref=send.at[c, far], dst_ref=recv.at[c, far], send_sem=dsend_sem.at[c], recv_sem=drecv_sem.at[c],
                                                 device_id=place(lax.rem(me + 1, n_dev)), device_id_type=pl.DeviceIdType.MESH)
        else:
            every = pltpu.make_async_remote_copy(src_ref=zsend.at[c, far], dst_ref=ret.at[c, far], send_sem=rsend_sem.at[c], recv_sem=rrecv_sem.at[c],
                                                 device_id=place(lax.rem(me + 1, n_dev)), device_id_type=pl.DeviceIdType.MESH)
        getattr(every, what)()

    for c in range(chunks):
        all_of(dispatch, c, 'start')
        pltpu.make_async_copy(send.at[c, me], recv.at[c, me], loc_sem.at[c]).start()

    for c in range(chunks):
        pltpu.make_async_copy(send.at[c, me], recv.at[c, me], loc_sem.at[c]).wait()
        all_of(dispatch, c, 'wait_recv')

        @pl.loop(0, n_dev)
        def _(dev):
            for s in range(slots):
                wide[pl.ds(pl.multiple_of((dev * slots + s) * sub, sub), sub), :] = recv[c, dev, s].astype(jnp.float32)

        for q in range(sub):
            xbuf[:, q * LANES:(q + 1) * LANES] = wide[pl.ds(q, rows, stride=sub), :].astype(jnp.bfloat16)

        @pl.loop(0, local_exp)
        def _(e):
            if c == 0:
                pltpu.make_async_copy(wgu.at[e], wgu.at[e], w_sem.at[0, e]).wait()
                pltpu.make_async_copy(wdv.at[e], wdv.at[e], w_sem.at[1, e]).wait()

            @pl.loop(0, gu_tiles)
            def _(j):
                both = jnp.dot(xbuf[...], wgu[e, j], preferred_element_type=jnp.float32)
                gate, up = both[:, :LANES], both[:, LANES:]
                act[:, pl.ds(pl.multiple_of(j * LANES, LANES), LANES)] = (gate * jax.nn.sigmoid(gate) * up).astype(jnp.bfloat16)

            @pl.loop(0, dn_tiles)
            def _(j):
                z = jnp.dot(act[...], wdv[e, j], preferred_element_type=jnp.float32)
                for i in range(dn_cols // LANES):
                    wide[pl.ds(j * (dn_cols // LANES) + i, rows, stride=sub), :] = z[:, i * LANES:(i + 1) * LANES]

            @pl.loop(0, n_dev)
            def _(dev):
                for s in range(slots):
                    zsend[c, dev, e, s] = wide[pl.ds(pl.multiple_of((dev * slots + s) * sub, sub), sub), :].astype(jnp.bfloat16)

        all_of(give_back, c, 'start')
        pltpu.make_async_copy(zsend.at[c, me], ret.at[c, me], loc_sem.at[chunks + c]).start()

    for c in range(chunks):
        pltpu.make_async_copy(zsend.at[c, me], ret.at[c, me], loc_sem.at[chunks + c]).wait()
        all_of(give_back, c, 'wait_recv')
    for c in range(chunks):
        all_of(dispatch, c, 'wait_send')
        all_of(give_back, c, 'wait_send')

    @pl.loop(0, tok_dev)
    def _(t):
        total = jnp.zeros((sub, LANES), jnp.float32)
        for k in range(top_k):
            at = pos_ref[t * top_k + k]
            dev_at = at // (local_exp * slots)
            rest = lax.rem(at, local_exp * slots)
            c_at = dev_at // n_dev
            total += gate_ref[t * top_k + k] * ret[c_at, lax.rem(dev_at, n_dev), rest // slots, lax.rem(rest, slots)].astype(jnp.float32)
        y_ref[t] = (h_ref[t].astype(jnp.float32) + total).astype(jnp.bfloat16)


def routing_tables(expert_idx, local_exp, n_dev, chunks):
    tok_dev, top_k = expert_idx.shape
    per_dev = tok_dev * top_k // (n_dev * local_exp)
    slots = per_dev // chunks
    dev = expert_idx // local_exp
    devs = jnp.arange(n_dev)
    member = jnp.any(dev[:, :, None] == devs[None, None, :], axis=1)
    before = (jnp.arange(tok_dev)[:, None] > jnp.arange(tok_dev)[None, :]).astype(jnp.bfloat16)
    slot_all = jnp.dot(before, member.astype(jnp.bfloat16), preferred_element_type=jnp.float32).astype(jnp.int32)
    slot = jnp.sum(jnp.where(dev[:, :, None] == devs[None, None, :], slot_all[:, None, :], 0), axis=2)
    here = member[:, :, None] & (slot_all[:, :, None] == jnp.arange(per_dev)[None, None, :])
    src = jnp.sum(jnp.where(here, jnp.arange(tok_dev, dtype=jnp.int32)[:, None, None], 0), axis=0)
    src = src.reshape(n_dev, chunks, slots).transpose(1, 0, 2).reshape(-1)
    pos = (((slot // slots) * n_dev + dev) * local_exp + expert_idx % local_exp) * slots + slot % slots
    return src, pos.reshape(-1)


def moe(h_tiles, expert_idx, gate_vals, w_gate, w_up, w_down, cp_devs, tp_devs, chunks=2):
    tok_dev, sub, _ = h_tiles.shape
    hidden = sub * LANES
    local_exp, _, ffn = w_gate.shape
    top_k = expert_idx.shape[1]
    n_dev = cp_devs * tp_devs
    slots = tok_dev * top_k // (n_dev * local_exp) // chunks
    rows = n_dev * slots
    gu_tiles, dn_cols = ffn // LANES, 2 * LANES
    dn_tiles = hidden // dn_cols
    src, pos = routing_tables(expert_idx, local_exp, n_dev, chunks)
    bf16, f32 = jnp.bfloat16, jnp.float32
    flops = 6 * chunks * rows * local_exp * hidden * ffn
    out = pl.pallas_call(
        functools.partial(moe_kernel, cp_devs, tp_devs, chunks),
        out_shape=jax.ShapeDtypeStruct((tok_dev, sub, LANES), bf16),
        in_specs=[pl.BlockSpec(memory_space=pltpu.SMEM)] * 3 + [pl.BlockSpec(memory_space=pltpu.VMEM)] + [pl.BlockSpec(memory_space=pl.ANY)] * 3,
        out_specs=pl.BlockSpec(memory_space=pltpu.VMEM),
        scratch_shapes=[
            pltpu.VMEM((chunks, n_dev, slots, sub, LANES), bf16),
            pltpu.VMEM((chunks, n_dev, slots, sub, LANES), bf16),
            pltpu.VMEM((rows, hidden), bf16),
            pltpu.VMEM((local_exp, gu_tiles, hidden, 2 * LANES), bf16),
            pltpu.VMEM((local_exp, dn_tiles, ffn, dn_cols), bf16),
            pltpu.VMEM((rows, ffn), bf16),
            pltpu.VMEM((rows * sub, LANES), f32),
            pltpu.VMEM((chunks, n_dev, local_exp, slots, sub, LANES), bf16),
            pltpu.VMEM((chunks, n_dev, local_exp, slots, sub, LANES), bf16),
            pltpu.SemaphoreType.DMA((2, local_exp)),
            pltpu.SemaphoreType.DMA((2 * chunks,)),
            pltpu.SemaphoreType.DMA((chunks,)),
            pltpu.SemaphoreType.DMA((chunks,)),
            pltpu.SemaphoreType.DMA((chunks,)),
            pltpu.SemaphoreType.DMA((chunks,)),
        ],
        compiler_params=pltpu.CompilerParams(collective_id=0, has_side_effects=True, vmem_limit_bytes=67043328),
        cost_estimate=pl.CostEstimate(flops=flops, bytes_accessed=6 * local_exp * hidden * ffn, transcendentals=rows * ffn),
        name='moe_exchange',
    )(src, pos, gate_vals.reshape(-1), h_tiles, w_gate, w_up, w_down)
    return out.reshape(tok_dev, hidden)


RING = 4
BATCHES = (((0, 0, 0), (0, 0, 1), (0, 1, 0), (0, 1, 1)),
           ((1, 0, 0), (1, 1, 0), (3, 0, 0), (3, 1, 0)),
           ((1, 0, 1), (1, 1, 1), (3, 0, 1), (3, 1, 1)),
           ((2, 0, 0), (2, 0, 1), (2, 1, 0), (2, 1, 1)))
SEND_ORDER = ((1, 0), (3, 0), (1, 1), (3, 1), (2, 0), (2, 1))


def attention_kernel(cp_devs, tp_devs, hid_ref, w_ref, wo_ref, h_ref,
                     xg, stage, q_all, kv_all, o_st, og, o_rows, wo_all, wide, acc, m_run, l_run,
                     xs_sem, xr_sem, fs_sem, fr_sem, ys_sem, yq_sem, ykv_sem, ks_sem, kr_sem, ws_sem, wr_sem, wfs_sem, wfr_sem, os_sem, or_sem):
    row, tp = lax.axis_index('cp'), lax.axis_index('tp')
    col, core = tp // CORES, lax.rem(tp, CORES)
    x_devs = tp_devs // CORES
    n_dev = cp_devs * tp_devs
    n_half, half_rows, hidden = hid_ref.shape
    units = tp_devs * n_half
    half_units = units // 2
    half_cp = cp_devs // 2
    batch_units = len(BATCHES[0])
    n_heads_loc = stage.shape[1]
    wo_rows = wo_ref.shape[0]
    f32, bf16 = jnp.float32, jnp.bfloat16
    mesh_id = pl.DeviceIdType.MESH
    sibling = {'cp': row, 'tp': col * CORES + 1 - core}

    def remote(src, dst, send_sem, recv_sem, dev):
        return pltpu.make_async_remote_copy(src_ref=src, dst_ref=dst, send_sem=send_sem, recv_sem=recv_sem, device_id=dev, device_id_type=mesh_id)

    def beside(d):
        return {'cp': row, 'tp': lax.rem(col + d, x_devs) * CORES + core}

    barrier = pltpu.get_barrier_semaphore()

    def greet(p, carry):
        dev = lax.rem(row * tp_devs + tp + p, n_dev)
        pl.semaphore_signal(barrier, inc=1, device_id={'cp': dev // tp_devs, 'tp': lax.rem(dev, tp_devs)}, device_id_type=mesh_id)
        return carry

    lax.fori_loop(1, n_dev, greet, 0)
    xg[0, 0] = hid_ref[0]
    xg[0, 1] = hid_ref[1]
    wo_all[pl.ds(pl.multiple_of(tp * wo_rows, wo_rows), wo_rows), :] = wo_ref[...]
    pl.semaphore_wait(barrier, n_dev - 1)

    where = {och: (b, u) for b, batch in enumerate(BATCHES) for u, och in enumerate(batch)}

    def direct(d, h):
        o = x_devs - d
        b, u = where[(o, 0, h)]
        return remote(hid_ref.at[h], xg.at[b, u], xs_sem.at[d - 1, h], xr_sem.at[o - 1, h], beside(d))

    def handed(o, h):
        b, u = where[(o, 0, h)]
        b2, u2 = where[(o, 1, h)]
        src = hid_ref.at[h] if o == 0 else xg.at[b, u]
        return remote(src, xg.at[b2, u2], fs_sem.at[o, h], fr_sem.at[o, h], sibling)

    for h in range(n_half):
        handed(0, h).start()
    for d, h in SEND_ORDER:
        direct(d, h).start()

    def unit_of(o, c, h):
        return (lax.rem(col + o, x_devs) * CORES + lax.rem(core + c, CORES)) * n_half + h

    def exchange(b):
        for i in range(n_heads_loc):
            to_row = core * n_heads_loc + i
            own = to_row == row
            for u, (o, c, h) in enumerate(BATCHES[b]):
                unit = unit_of(o, c, h)
                for kind, src, dst, sem in ((0, stage.at[b, i, u, 0], q_all.at[lax.rem(row, half_cp), unit], yq_sem),
                                            (1, stage.at[b, i, u, pl.ds(1, 2)], kv_all.at[row, unit], ykv_sem)):
                    got = sem.at[lax.rem(row, half_cp), b]

                    @pl.when(own)
                    def _():
                        pltpu.make_async_copy(src, dst, got).start()

                    @pl.when(jnp.logical_not(own))
                    def _():
                        remote(src, dst, ys_sem.at[kind, i], got, {'cp': to_row, 'tp': col * CORES + row // half_cp}).start()

    def share(b):
        for rr in range(half_cp):
            r = core * half_cp + rr
            some = pl.ds(0, batch_units)
            pltpu.make_async_copy(kv_all.at[r, some], kv_all.at[r, some], ykv_sem.at[rr, b]).wait()
            for o, c, h in BATCHES[b]:
                unit = unit_of(o, c, h)
                remote(kv_all.at[r, unit], kv_all.at[r, unit], ks_sem, kr_sem.at[rr, b], sibling).start()

    for b in range(len(BATCHES)):
        for o, c, h in BATCHES[b]:
            if c == 0 and o:
                direct(x_devs - o, h).wait_recv()
                handed(o, h).start()
        for o, c, h in BATCHES[b]:
            if c == 1:
                handed(o, h).wait_recv()

        @pl.loop(0, 3)
        def _(n):
            y = jnp.dot(xg[b].reshape(batch_units * half_rows, hidden), w_ref[n], preferred_element_type=f32).astype(bf16)
            for i in range(n_heads_loc):
                for u in range(batch_units):
                    stage[b, i, u, n] = y[u * half_rows:(u + 1) * half_rows, i * LANES:(i + 1) * LANES]

        exchange(b)
        if b:
            share(b - 1)
    share(len(BATCHES) - 1)

    def wo_part(t):
        return wo_all.at[pl.ds(pl.multiple_of(t * wo_rows, wo_rows), wo_rows)]

    def wo_direct(d):
        return remote(wo_ref, wo_part(tp), ws_sem.at[d - 1], wr_sem.at[x_devs - d - 1], beside(d))

    def wo_from(o):
        t = lax.rem(col + o, x_devs) * CORES + core
        return remote(wo_ref, wo_part(t), ws_sem.at[x_devs - o - 1], wr_sem.at[o - 1], beside(x_devs - o))

    def wo_handed(o):
        t = lax.rem(col + o, x_devs) * CORES + core
        return remote(wo_ref if o == 0 else wo_part(t), wo_part(t), wfs_sem.at[o], wfr_sem.at[o], sibling)

    for d in (1, 3, 2):
        wo_direct(d).start()
    wo_handed(0).start()

    for rr in range(half_cp):
        for b in range(len(BATCHES)):
            some = pl.ds(0, batch_units)
            pltpu.make_async_copy(q_all.at[rr, some], q_all.at[rr, some], yq_sem.at[rr, b]).wait()
            other = (1 - core) * half_cp + rr
            remote(kv_all.at[other, some], kv_all.at[other, some], ks_sem, kr_sem.at[rr, b], sibling).wait_recv()

    scale = LANES ** -0.5 * math.log2(math.e)
    sub_units = half_units // 2
    sub_rows = sub_units * half_rows
    repeat = half_units * half_rows // LANES
    head = col * cp_devs + row

    def scores(q, keys):
        return lax.dot_general(q, keys, (((1,), (1,)), ((), ())), preferred_element_type=f32) * scale

    def lane_sums(p):
        total = p[:, :LANES]
        for i in range(1, p.shape[1] // LANES):
            total += p[:, i * LANES:(i + 1) * LANES]
        return total

    @pl.loop(0, 2 * half_cp)
    def _(piece):
        rr, late = piece // 2, lax.rem(piece, 2)
        block = core * half_cp + rr
        place = jnp.where(late == 0, block, 2 * cp_devs - 1 - block)
        for sub in range(2):
            q = q_all[rr, pl.ds(late * half_units + sub * sub_units, sub_units)].reshape(sub_rows, LANES)
            near = (sub + 1) * sub_units
            keys = kv_all[block, pl.ds(late * half_units, near), 0].reshape(near * half_rows, LANES)
            vals = kv_all[block, pl.ds(late * half_units, near), 1].reshape(near * half_rows, LANES)
            s = scores(q, keys)
            q_at = sub * sub_rows + lax.broadcasted_iota(jnp.int32, s.shape, 0)
            s = jnp.where(lax.broadcasted_iota(jnp.int32, s.shape, 1) <= q_at, s, -1e30)
            m = jnp.broadcast_to(jnp.max(s, axis=1, keepdims=True), (sub_rows, LANES))
            p = jnp.exp2(s - jnp.concatenate([m] * (s.shape[1] // LANES), axis=1))
            m_run[...] = m
            l_run[...] = lane_sums(p)
            acc[...] = jnp.dot(p.astype(bf16), vals, preferred_element_type=f32)

            @pl.loop(0, place)
            def _(kp):
                k_block = jnp.where(kp < cp_devs, kp, 2 * cp_devs - 1 - kp)
                k_first = jnp.where(kp < cp_devs, 0, half_units)
                keys = kv_all[k_block, pl.ds(k_first, half_units), 0].reshape(half_units * half_rows, LANES)
                vals = kv_all[k_block, pl.ds(k_first, half_units), 1].reshape(half_units * half_rows, LANES)
                s = scores(q_all[rr, pl.ds(late * half_units + sub * sub_units, sub_units)].reshape(sub_rows, LANES), keys)
                before = m_run[...]
                m = jnp.maximum(before, jnp.max(s, axis=1, keepdims=True))
                p = jnp.exp2(s - jnp.concatenate([m] * repeat, axis=1))
                fade = jnp.exp2(before - m)
                m_run[...] = m
                l_run[...] = fade * l_run[...] + lane_sums(p)
                acc[...] = fade * acc[...] + jnp.dot(p.astype(bf16), vals, preferred_element_type=f32)

            o = acc[...] / jnp.sum(l_run[...], axis=1, keepdims=True)
            o_st[rr, pl.ds(late * half_units + sub * sub_units, sub_units)] = o.astype(bf16).reshape(sub_units, half_rows, LANES)

        for t in range(tp_devs // 2):
            to_tp = late * (tp_devs // 2) + t
            src = o_st.at[rr, pl.ds(to_tp * n_half, n_half)]
            own = jnp.logical_and(block == row, to_tp == tp)

            @pl.when(own)
            def _():
                pltpu.make_async_copy(src, og.at[head], or_sem).start()

            @pl.when(jnp.logical_not(own))
            def _():
                remote(src, og.at[head], os_sem, or_sem, {'cp': block, 'tp': to_tp}).start()

        @pl.when(piece == 1)
        def _():
            for o in (1, 3):
                wo_from(o).wait_recv()
                wo_handed(o).start()

    wo_from(2).wait_recv()
    wo_handed(2).start()
    pltpu.make_async_copy(og, og, or_sem).wait()
    for n in range(og.shape[0]):
        o_rows[:, n * LANES:(n + 1) * LANES] = og[n].reshape(n_half * half_rows, LANES)
    for o in range(x_devs):
        t = lax.rem(col + o, x_devs) * CORES + 1 - core
        remote(wo_part(t), wo_part(t), wfs_sem.at[o], wfr_sem.at[o], sibling).wait_recv()

    sub = hidden // LANES
    step = 2 * LANES
    rows = n_half * half_rows

    @pl.loop(0, hidden // step)
    def _(j):
        cols = pl.ds(pl.multiple_of(j * step, step), step)
        h = jnp.dot(o_rows[...], wo_all[:, cols], preferred_element_type=f32) + hid_ref[:, :, cols].reshape(rows, step).astype(f32)
        for i in range(step // LANES):
            wide[pl.ds(j * (step // LANES) + i, rows, stride=sub), :] = h[:, i * LANES:(i + 1) * LANES]

    @pl.loop(0, rows // 8)
    def _(t):
        for i in range(8):
            h_ref[t * 8 + i] = wide[pl.ds(pl.multiple_of((t * 8 + i) * sub, sub), sub), :].astype(bf16)

    for d, h in SEND_ORDER:
        direct(d, h).wait_send()
    for o in range(x_devs):
        for h in range(n_half):
            handed(o, h).wait_send()
        wo_handed(o).wait_send()
    for d in range(1, x_devs):
        wo_direct(d).wait_send()
    for i in range(n_heads_loc):
        @pl.when(core * n_heads_loc + i != row)
        def _():
            remote(q_all.at[0], q_all.at[0], ys_sem.at[0, i], yq_sem.at[0, 0], sibling).wait_send()
            remote(kv_all.at[0], kv_all.at[0], ys_sem.at[1, i], ykv_sem.at[0, 0], sibling).wait_send()
    every = kv_all.at[pl.ds(0, half_cp)]
    remote(every, every, ks_sem, kr_sem.at[0, 0], sibling).wait_send()
    own_row = row // half_cp == core

    @pl.when(own_row)
    def _():
        most = og.at[pl.ds(0, og.shape[0] - 1)]
        remote(most, most, os_sem, or_sem, sibling).wait_send()

    @pl.when(jnp.logical_not(own_row))
    def _():
        remote(og, og, os_sem, or_sem, sibling).wait_send()


def attention_residual(hidden_in, w_query, w_key, w_value, w_out, cp_devs, tp_devs):
    tok_dev, hidden = hidden_in.shape
    heads_loc, head_dim = w_query.shape[1:]
    if w_key.shape != w_query.shape or head_dim != LANES or tp_devs != RING * CORES or heads_loc * CORES != cp_devs:
        raise ValueError('unexpected sizes')
    n_half = 2
    half_rows = tok_dev // n_half
    units = tp_devs * n_half
    n_heads = heads_loc * tp_devs
    batches, batch_units = len(BATCHES), len(BATCHES[0])
    half_cp = cp_devs // 2
    sub = hidden // LANES
    sub_rows = units // 4 * half_rows
    bf16, f32 = jnp.bfloat16, jnp.float32
    dma = pltpu.SemaphoreType.DMA
    w_all = jnp.stack([w.reshape(hidden, heads_loc * head_dim) for w in (w_query, w_key, w_value)])
    return pl.pallas_call(
        functools.partial(attention_kernel, cp_devs, tp_devs),
        out_shape=jax.ShapeDtypeStruct((tok_dev, sub, LANES), bf16),
        in_specs=[pl.BlockSpec(memory_space=pltpu.VMEM)] * 3,
        out_specs=pl.BlockSpec(memory_space=pltpu.VMEM),
        scratch_shapes=[
            pltpu.VMEM((batches, batch_units, half_rows, hidden), bf16),
            pltpu.VMEM((batches, heads_loc, batch_units, 3, half_rows, LANES), bf16),
            pltpu.VMEM((half_cp, units, half_rows, LANES), bf16),
            pltpu.VMEM((cp_devs, units, 2, half_rows, LANES), bf16),
            pltpu.VMEM((half_cp, units, half_rows, LANES), bf16),
            pltpu.VMEM((n_heads, n_half, half_rows, LANES), bf16),
            pltpu.VMEM((tok_dev, hidden), bf16),
            pltpu.VMEM((n_heads * head_dim, hidden), bf16),
            pltpu.VMEM((tok_dev * sub, LANES), f32),
            pltpu.VMEM((sub_rows, LANES), f32),
            pltpu.VMEM((sub_rows, LANES), f32),
            pltpu.VMEM((sub_rows, LANES), f32),
            dma((RING - 1, n_half)), dma((RING - 1, n_half)), dma((RING, n_half)), dma((RING, n_half)),
            dma((2, heads_loc)), dma((half_cp, batches)), dma((half_cp, batches)), dma, dma((half_cp, batches)),
            dma((RING - 1,)), dma((RING - 1,)), dma((RING,)), dma((RING,)), dma, dma,
        ],
        compiler_params=pltpu.CompilerParams(collective_id=1, has_side_effects=True, vmem_limit_bytes=67043328),
        cost_estimate=pl.CostEstimate(flops=12 * 10 ** 9, bytes_accessed=16 * 10 ** 6, transcendentals=10 ** 7),
        name='attention_exchange',
    )(hidden_in.reshape(n_half, half_rows, hidden), w_all, w_out.reshape(heads_loc * head_dim, hidden))


from jax.sharding import PartitionSpec as P


def solution(mesh):
    cp_devs, tp_devs = mesh.shape['cp'], mesh.shape['tp']
    row_spec = P(('dp', 'cp', 'tp'), None)
    head_spec = P(None, 'tp', None)
    expert_spec = P(('cp', 'tp'), None, None)

    def device_step(hidden_in, w_query, w_key, w_value, w_out, expert_idx, gate_vals, w_gate, w_up, w_down):
        h_tiles = attention_residual(hidden_in, w_query, w_key, w_value, w_out, cp_devs, tp_devs)
        return moe(h_tiles, expert_idx, gate_vals, w_gate, w_up, w_down, cp_devs, tp_devs)

    return jax.shard_map(device_step, mesh=mesh, in_specs=(row_spec, head_spec, head_spec, head_spec, P('tp', None, None), row_spec, row_spec, expert_spec, expert_spec, expert_spec), out_specs=row_spec, check_vma=False)
```

time: 559 us -> 273 us (0.49); the launches traced: 550 us -> 271 us
  Pallas kernels: 0 us -> 257 us
  waiting for transfers between devices: 211 us -> 0 us
  matrix products: 117 us -> 0.15 us
  blocking collectives: 71.1 us -> 0 us
  local copies, waits for them, and re-layouts: 79.9 us -> 9.61 us
  other arithmetic: 50.9 us -> 4.01 us
  between operations: 13.9 us -> 0.09 us
    pallas_call x0 -> x2, Pallas kernels: none -> 257 us  [the longest x1 130 us: attention_residual(): pl.pallas_call(functools.partial(attention_kernel, cp_devs, tp_devs), out...]
    dot_general x31 -> x1, matrix products: 117 us -> 0.15 us  [routing_tables(): jnp.dot(before, member.astype(jnp.bfloat16), preferred_element_type=jnp.f...]
    all_gather x3 -> x0, waiting for transfers between devices: 104 us -> none  [the longest x1 43.9 us: attention_residual(): gathered = lax.all_gather(hidden_in, 'tp', axis=0, tiled=True)]
    all_to_all x1 -> x0, blocking collectives: 71.1 us -> none  [device_step(): recv_buf = lax.all_to_all(send_buf, ('cp', 'tp'), 0, 0, tiled=True)]
    all_to_all x1 -> x0, waiting for transfers between devices: 63.8 us -> none  [device_step(): lax.all_to_all(expert_out.reshape(experts * capacity, hidden), ('cp', 'tp...]
    reduce_scatter x1 -> x0, waiting for transfers between devices: 42.8 us -> none  [attention_residual(): reduced = lax.psum_scatter(part_sum, 'tp', scatter_dimension=0, tiled=True)]
    gather x4 -> x0, local copies, waits for them, and re-layouts: 35.3 us -> none  [the longest x2 22.1 us: device_step(): jnp.take(returned, dest_row, axis=0).reshape(tok_dev, top_k, hidden)]
    reduce_sum x14 -> x2, other arithmetic: 20.5 us -> 0.45 us  [the longest x1 0.41 us: routing_tables(): jnp.sum(jnp.where(here, jnp.arange(tok_dev, dtype=jnp.int32)[:, None, Non...]
  transfers between devices with their start and end apart: 5 -> 0, of which waited for: 5 -> 0; matrix products, arithmetic and copies ran while one was open for 8% -> 0% of each run, Pallas kernels for 0% -> 0%
where the time goes in v1:
time: 273 us; the launch traced here: 271 us
  Pallas kernels  257 us (94%)
  local copies, waits for them, and re-layouts  9.61 us (4%)
  other arithmetic  4.01 us (1%)
    pallas_call x1, Pallas kernels, attention_residual(): pl.pallas_call(functools.partial(attention_kernel, cp_devs, tp_devs), out...  130 us
    pallas_call x1, Pallas kernels, moe(): pl.pallas_call(functools.partial(moe_kernel, cp_devs, tp_devs, chunks), o...  128 us

profile of v1, /device:TPU:97, one launch (start us, length us, event | category | flops | bytes accessed | tf_op | source)
XLA Modules:
  0.0 271.3 jit_solution(7044278000109032118)
XLA Ops:
  0.0 0.0 copy-start
  0.0 0.8 add_select_fusion.3
  0.8 0.2 convolution_convert_fusion
  1.0 0.4 select_reduce_fusion
  1.4 0.1 copy.20
  1.5 0.7 reshape.26.src_ref
  2.3 0.7 fusion.7
  3.0 0.1 copy.21
  3.1 0.7 reshape.27.pos_ref
  3.9 1.7 stack_reshape.10
  5.6 0.0 copy-done
  5.6 0.7 stack_reshape.11
  6.3 1.7 stack_reshape.9
  8.1 2.0 pad_maximum_fusion.w_ref
  10.1 129.7 %attention_exchange.1.h_ref = bf16[192,16,128]{2,1,0:T(8,128)(2,1)} custom-call(bf16[2,96,2048]{2,1,0:T(8,128)(2,1)} %bitcast.13, bf16[3,2048,256]{2,1,0:T(8,128)(2,1)} %pad_maximum_fusion.w_ref, bf16[256,2048]{1,0:T(8,128)(2,1)} %bitcast.12), custom_call_target="tpu_custom_call" | custom-call | flops 12000000000 | bytes 16000000 | tf_op jit(solution)/shard_map/attention_exchange/pallas_call | solution.py:498
  139.8 0.8 copy.22
  140.6 0.7 reshape.28.gate_ref
  141.3 127.7 %moe_exchange.1 = bf16[192,16,128]{2,1,0:T(8,128)(2,1)} custom-call(s32[576]{0:T(1024)} %reshape.26.src_ref, s32[1152]{0:T(1024)} %reshape.27.pos_ref, f32[1152]{0:T(1024)} %reshape.28.gate_ref, bf16[192,16,128]{2,1,0:T(8,128)(2,1)} %attention_exchange.1.h_ref, bf16[2,2048,1408]{2,1,0:T(8,128)(2,1)} %wg_ref.1, bf16[2,2048,1408]{2,1,0:T(8,128)(2,1)} %wu_ref.1, ...), custom_call_target="tpu_custom_call" | custom-call | flops 19931332608 | bytes 34603008 | tf_op jit(solution)/shard_map/moe_exchange/pallas_call | solution.py:191
  269.1 2.2 copy.25
  (3 shorter events, 0.1 us)
Async XLA Ops:
  0.0 5.6 %copy-start = (bf16[2048,2,128]{2,1,0:T(2,128)(2,1)S(1)}, bf16[2048,2,128]{2,1,0:T(2,128)(2,1)}, u32[]{:S(2)}) copy-start(bf16[2048,2,128]{2,1,0:T(2,128)(2,1)} %param.13) | copy-start | bytes 3145732

commit v2 on v1

v2 whole, which is shorter than its diff:
```python
import functools
import math
import jax
import jax.numpy as jnp
from jax import lax
from jax.experimental import pallas as pl
from jax.experimental.pallas import tpu as pltpu

LANES = 128
VMEM_BYTES = 66 * 1024 * 1024


CORES = 2


def spread_order(cp_devs, tp_devs):
    x_devs = tp_devs // CORES
    row, col = lax.axis_index('cp'), lax.axis_index('tp') // CORES
    core = lax.rem(lax.axis_index('tp'), CORES)
    hops = lambda d, n: min(d, n - d)
    chips = [(dx, dy) for dx in range(x_devs) for dy in range(cp_devs)]
    chips.sort(key=lambda o: (-(hops(o[0], x_devs) + hops(o[1], cp_devs)), abs(hops(o[0], x_devs) - hops(o[1], cp_devs)), (o[0] * 3 + o[1] * 5) % 4))
    for dc in range(CORES):
        for dx, dy in chips:
            if dx or dy or dc:
                yield lax.rem(row + dy, cp_devs) * tp_devs + lax.rem(col + dx, x_devs) * CORES + lax.rem(core + dc, CORES)


def moe_kernel(cp_devs, tp_devs, chunks, src_ref, pos_ref, gate_ref, h_ref, wg_ref, wu_ref, wd_ref, y_ref,
               send, recv, xbuf, wgu, wdv, act, wide, zsend, ret, w_sem, loc_sem, dsend_sem, drecv_sem, rsend_sem, rrecv_sem):
    n_dev = cp_devs * tp_devs
    local_exp = wg_ref.shape[0]
    tok_dev, sub = h_ref.shape[0], h_ref.shape[1]
    slots = send.shape[2]
    rows = n_dev * slots
    gu_tiles, dn_tiles = wgu.shape[1], wdv.shape[1]
    dn_cols = wdv.shape[3]
    top_k = gate_ref.shape[0]
    back = local_exp * slots
    me = lax.axis_index('cp') * tp_devs + lax.axis_index('tp')

    def place(dev):
        return {'cp': dev // tp_devs, 'tp': lax.rem(dev, tp_devs)}

    barrier = pltpu.get_barrier_semaphore()

    def greet(p, carry):
        pl.semaphore_signal(barrier, inc=1, device_id=place(lax.rem(me + p, n_dev)), device_id_type=pl.DeviceIdType.MESH)
        return carry

    lax.fori_loop(1, n_dev, greet, 0)

    def gu_copy(e, j, half, ref):
        return pltpu.make_async_copy(ref.at[e, :, pl.ds(pl.multiple_of(j * LANES, LANES), LANES)],
                                     wgu.at[e, j, :, pl.ds(half * LANES, LANES)], w_sem.at[0, e])

    def dn_copy(e, j):
        return pltpu.make_async_copy(wd_ref.at[e, :, pl.ds(pl.multiple_of(j * dn_cols, dn_cols), dn_cols)], wdv.at[e, j], w_sem.at[1, e])

    for e in range(local_exp):
        @pl.loop(0, gu_tiles)
        def _(j):
            gu_copy(e, j, 0, wg_ref).start()
            gu_copy(e, j, 1, wu_ref).start()

        @pl.loop(0, dn_tiles)
        def _(j):
            dn_copy(e, j).start()

    def fill(dev, carry):
        for c in range(chunks):
            for s in range(slots):
                send[c, dev, s] = h_ref[src_ref[c * slots + s, dev]]
        return carry

    with jax.named_scope('m_fill'):
        lax.fori_loop(0, n_dev, fill, 0)
    with jax.named_scope('m_barrier'):
        pl.semaphore_wait(barrier, n_dev - 1)

    def dispatch(c, dev):
        return pltpu.make_async_remote_copy(src_ref=send.at[c, dev], dst_ref=recv.at[c, me], send_sem=dsend_sem.at[c], recv_sem=drecv_sem.at[c],
                                            device_id=place(dev), device_id_type=pl.DeviceIdType.MESH)

    def give_back(c, dev):
        return pltpu.make_async_remote_copy(src_ref=zsend.at[c, dev], dst_ref=ret.at[pl.ds((c * n_dev + me) * back, back)], send_sem=rsend_sem.at[c], recv_sem=rrecv_sem.at[c],
                                            device_id=place(dev), device_id_type=pl.DeviceIdType.MESH)

    def all_of(copy, c, what):
        if what == 'start':
            for dev in spread_order(cp_devs, tp_devs):
                copy(c, dev).start()
            return
        far = pl.ds(0, n_dev - 1)
        if copy is dispatch:
            every = pltpu.make_async_remote_copy(src_ref=send.at[c, far], dst_ref=recv.at[c, far], send_sem=dsend_sem.at[c], recv_sem=drecv_sem.at[c],
                                                 device_id=place(lax.rem(me + 1, n_dev)), device_id_type=pl.DeviceIdType.MESH)
        else:
            every = pltpu.make_async_remote_copy(src_ref=zsend.at[c, far], dst_ref=zsend.at[c, far], send_sem=rsend_sem.at[c], recv_sem=rrecv_sem.at[c],
                                                 device_id=place(lax.rem(me + 1, n_dev)), device_id_type=pl.DeviceIdType.MESH)
        getattr(every, what)()

    for c in range(chunks):
        with jax.named_scope('m_dstart'):
            all_of(dispatch, c, 'start')
        pltpu.make_async_copy(send.at[c, me], recv.at[c, me], loc_sem.at[c]).start()

    for c in range(chunks):
        pltpu.make_async_copy(send.at[c, me], recv.at[c, me], loc_sem.at[c]).wait()
        with jax.named_scope('m_dwait'):
            all_of(dispatch, c, 'wait_recv')

        with jax.named_scope('m_relay'):
            @pl.loop(0, n_dev)
            def _(dev):
                for s in range(slots):
                    wide[pl.ds(pl.multiple_of((dev * slots + s) * sub, sub), sub), :] = recv[c, dev, s].astype(jnp.float32)

            for q in range(sub):
                xbuf[:, q * LANES:(q + 1) * LANES] = wide[pl.ds(q, rows, stride=sub), :].astype(jnp.bfloat16)

        @pl.loop(0, local_exp)
        def _(e):
            if c == 0:
                with jax.named_scope('m_wwait'):
                    pltpu.make_async_copy(wgu.at[e], wgu.at[e], w_sem.at[0, e]).wait()
                    pltpu.make_async_copy(wdv.at[e], wdv.at[e], w_sem.at[1, e]).wait()

            with jax.named_scope('m_gu'):
                @pl.loop(0, gu_tiles)
                def _(j):
                    both = jnp.dot(xbuf[...], wgu[e, j], preferred_element_type=jnp.float32)
                    gate, up = both[:, :LANES], both[:, LANES:]
                    act[:, pl.ds(pl.multiple_of(j * LANES, LANES), LANES)] = (gate * jax.nn.sigmoid(gate) * up).astype(jnp.bfloat16)

            with jax.named_scope('m_dn'):
                @pl.loop(0, dn_tiles)
                def _(j):
                    z = jnp.dot(act[...], wdv[e, j], preferred_element_type=jnp.float32)
                    for i in range(dn_cols // LANES):
                        wide[pl.ds(j * (dn_cols // LANES) + i, rows, stride=sub), :] = z[:, i * LANES:(i + 1) * LANES]

            with jax.named_scope('m_pack'):
                @pl.loop(0, n_dev)
                def _(dev):
                    for s in range(slots):
                        zsend[c, dev, e * slots + s] = wide[pl.ds(pl.multiple_of((dev * slots + s) * sub, sub), sub), :].astype(jnp.bfloat16)

        with jax.named_scope('m_rstart'):
            all_of(give_back, c, 'start')
        pltpu.make_async_copy(zsend.at[c, me], ret.at[pl.ds((c * n_dev + me) * back, back)], loc_sem.at[chunks + c]).start()

    for c in range(chunks):
        pltpu.make_async_copy(zsend.at[c, me], ret.at[pl.ds((c * n_dev + me) * back, back)], loc_sem.at[chunks + c]).wait()
        with jax.named_scope('m_rwait'):
            all_of(give_back, c, 'wait_recv')
    for c in range(chunks):
        with jax.named_scope('m_drain'):
            all_of(dispatch, c, 'wait_send')
            all_of(give_back, c, 'wait_send')

    with jax.named_scope('m_combine'):
        group = 8

        @pl.loop(0, tok_dev // group)
        def _(g):
            for i in range(group):
                t = g * group + i
                total = gate_ref[0, t] * ret[pos_ref[0, t]].astype(jnp.float32)
                for k in range(1, top_k):
                    total += gate_ref[k, t] * ret[pos_ref[k, t]].astype(jnp.float32)
                wide[pl.ds(pl.multiple_of(t * sub, sub), sub), :] = h_ref[t].astype(jnp.float32) + total

        for q in range(sub):
            y_ref[:, q * LANES:(q + 1) * LANES] = wide[pl.ds(q, tok_dev, stride=sub), :].astype(jnp.bfloat16)


def routing_tables(expert_idx, local_exp, n_dev, chunks):
    tok_dev, top_k = expert_idx.shape
    per_dev = tok_dev * top_k // (n_dev * local_exp)
    slots = per_dev // chunks
    dev = expert_idx // local_exp
    devs = jnp.arange(n_dev)
    member = jnp.any(dev[:, :, None] == devs[None, None, :], axis=1)
    before = (jnp.arange(tok_dev)[:, None] > jnp.arange(tok_dev)[None, :]).astype(jnp.bfloat16)
    slot_all = jnp.dot(before, member.astype(jnp.bfloat16), preferred_element_type=jnp.float32).astype(jnp.int32)
    slot = jnp.sum(jnp.where(dev[:, :, None] == devs[None, None, :], slot_all[:, None, :], 0), axis=2)
    here = member[:, :, None] & (slot_all[:, :, None] == jnp.arange(per_dev)[None, None, :])
    src = jnp.sum(jnp.where(here, jnp.arange(tok_dev, dtype=jnp.int32)[:, None, None], 0), axis=0)
    pos = (((slot // slots) * n_dev + dev) * local_exp + expert_idx % local_exp) * slots + slot % slots
    return src.T, pos.T


def moe(h_tiles, expert_idx, gate_vals, w_gate, w_up, w_down, cp_devs, tp_devs, chunks=3):
    tok_dev, sub, _ = h_tiles.shape
    hidden = sub * LANES
    local_exp, _, ffn = w_gate.shape
    top_k = expert_idx.shape[1]
    n_dev = cp_devs * tp_devs
    slots = tok_dev * top_k // (n_dev * local_exp) // chunks
    rows = n_dev * slots
    gu_tiles, dn_cols = ffn // LANES, 2 * LANES
    dn_tiles = hidden // dn_cols
    src, pos = routing_tables(expert_idx, local_exp, n_dev, chunks)
    bf16, f32 = jnp.bfloat16, jnp.float32
    flops = 6 * chunks * rows * local_exp * hidden * ffn
    out = pl.pallas_call(
        functools.partial(moe_kernel, cp_devs, tp_devs, chunks),
        out_shape=jax.ShapeDtypeStruct((tok_dev, hidden), bf16),
        in_specs=[pl.BlockSpec(memory_space=pltpu.SMEM)] * 3 + [pl.BlockSpec(memory_space=pltpu.VMEM)] + [pl.BlockSpec(memory_space=pl.ANY)] * 3,
        out_specs=pl.BlockSpec(memory_space=pltpu.VMEM),
        scratch_shapes=[
            pltpu.VMEM((chunks, n_dev, slots, sub, LANES), bf16),
            pltpu.VMEM((chunks, n_dev, slots, sub, LANES), bf16),
            pltpu.VMEM((rows, hidden), bf16),
            pltpu.VMEM((local_exp, gu_tiles, hidden, 2 * LANES), bf16),
            pltpu.VMEM((local_exp, dn_tiles, ffn, dn_cols), bf16),
            pltpu.VMEM((rows, ffn), bf16),
            pltpu.VMEM((max(rows, tok_dev) * sub, LANES), f32),
            pltpu.VMEM((chunks, n_dev, local_exp * slots, sub, LANES), bf16),
            pltpu.VMEM((chunks * n_dev * local_exp * slots, sub, LANES), bf16),
            pltpu.SemaphoreType.DMA((2, local_exp)),
            pltpu.SemaphoreType.DMA((2 * chunks,)),
            pltpu.SemaphoreType.DMA((chunks,)),
            pltpu.SemaphoreType.DMA((chunks,)),
            pltpu.SemaphoreType.DMA((chunks,)),
            pltpu.SemaphoreType.DMA((chunks,)),
        ],
        compiler_params=pltpu.CompilerParams(collective_id=0, has_side_effects=True, vmem_limit_bytes=67043328),
        cost_estimate=pl.CostEstimate(flops=flops, bytes_accessed=6 * local_exp * hidden * ffn, transcendentals=rows * ffn),
        name='moe_exchange',
    )(src, pos, gate_vals.T, h_tiles, w_gate, w_up, w_down)
    return out


RING = 4
BATCHES = (((0, 0, 0), (0, 0, 1), (0, 1, 0), (0, 1, 1)),
           ((3, 0, 0), (3, 1, 0), (1, 0, 1), (1, 1, 1)),
           ((3, 0, 1), (3, 1, 1), (1, 0, 0), (1, 1, 0)),
           ((2, 0, 0), (2, 0, 1), (2, 1, 0), (2, 1, 1)))
SEND_ORDER = ((1, 0), (3, 1), (1, 1), (3, 0))
ONWARD = {(3, 0): 1, (1, 1): 3}


def attention_kernel(cp_devs, tp_devs, hid_ref, wq_ref, wk_ref, wv_ref, wo_ref, h_ref,
                     w_in, xg, stage, q_all, kv_all, o_st, og, o_rows, wo_all, wide, acc, m_run, l_run,
                     xs_sem, xr_sem, fs_sem, fr_sem, ys_sem, yq_sem, ykv_sem, ks_sem, kr_sem, ws_sem, wr_sem, wfs_sem, wfr_sem, os_sem, or_sem, in_sem):
    row, tp = lax.axis_index('cp'), lax.axis_index('tp')
    col, core = tp // CORES, lax.rem(tp, CORES)
    x_devs = tp_devs // CORES
    n_dev = cp_devs * tp_devs
    n_half, half_rows, hidden = hid_ref.shape
    units = tp_devs * n_half
    half_units = units // 2
    half_cp = cp_devs // 2
    batch_units = len(BATCHES[0])
    n_heads_loc = stage.shape[1]
    wo_rows = wo_ref.shape[0]
    f32, bf16 = jnp.float32, jnp.bfloat16
    mesh_id = pl.DeviceIdType.MESH
    sibling = {'cp': row, 'tp': col * CORES + 1 - core}

    def remote(src, dst, send_sem, recv_sem, dev):
        return pltpu.make_async_remote_copy(src_ref=src, dst_ref=dst, send_sem=send_sem, recv_sem=recv_sem, device_id=dev, device_id_type=mesh_id)

    def beside(d):
        return {'cp': row, 'tp': lax.rem(col + d, x_devs) * CORES + core}

    barrier = pltpu.get_barrier_semaphore()

    def greet(p, carry):
        dev = lax.rem(row * tp_devs + tp + p, n_dev)
        pl.semaphore_signal(barrier, inc=1, device_id={'cp': dev // tp_devs, 'tp': lax.rem(dev, tp_devs)}, device_id_type=mesh_id)
        return carry

    lax.fori_loop(1, n_dev, greet, 0)
    loads = [pltpu.make_async_copy(ref, w_in.at[n], in_sem.at[n]) for n, ref in enumerate((wq_ref, wk_ref, wv_ref))]
    loads.append(pltpu.make_async_copy(wo_ref, wo_all.at[pl.ds(pl.multiple_of(tp * wo_rows, wo_rows), wo_rows)], in_sem.at[3]))
    for load in loads:
        load.start()
    xg[0, 0] = hid_ref[0]
    xg[0, 1] = hid_ref[1]
    with jax.named_scope('a_barrier'):
        pl.semaphore_wait(barrier, n_dev - 1)

    where = {och: (b, u) for b, batch in enumerate(BATCHES) for u, och in enumerate(batch)}

    def direct(d, h):
        o = x_devs - d
        b, u = where[(o, 0, h)]
        return remote(hid_ref.at[h], xg.at[b, u], xs_sem.at[d - 1, h], xr_sem.at[o - 1, h], beside(d))

    def onward(h):
        o = 3 if h == 0 else 1
        b, u = where[(o, 0, h)]
        b2, u2 = where[(2, 0, h)]
        return remote(xg.at[b, u], xg.at[b2, u2], xs_sem.at[1, h], xr_sem.at[1, h], beside(ONWARD[(o, h)]))

    def handed(o, h):
        b, u = where[(o, 0, h)]
        b2, u2 = where[(o, 1, h)]
        src = hid_ref.at[h] if o == 0 else xg.at[b, u]
        return remote(src, xg.at[b2, u2], fs_sem.at[o, h], fr_sem.at[o, h], sibling)

    for h in range(n_half):
        handed(0, h).start()
    for d, h in SEND_ORDER:
        direct(d, h).start()

    def unit_of(o, c, h):
        return (lax.rem(col + o, x_devs) * CORES + lax.rem(core + c, CORES)) * n_half + h

    def exchange(b):
        for i in range(n_heads_loc):
            to_row = core * n_heads_loc + i
            own = to_row == row
            for u, (o, c, h) in enumerate(BATCHES[b]):
                unit = unit_of(o, c, h)
                for kind, src, dst, sem in ((0, stage.at[b, i, u, 0], q_all.at[lax.rem(row, half_cp), unit], yq_sem),
                                            (1, stage.at[b, i, u, pl.ds(1, 2)], kv_all.at[row, unit], ykv_sem)):
                    got = sem.at[lax.rem(row, half_cp), b]

                    @pl.when(own)
                    def _():
                        pltpu.make_async_copy(src, dst, got).start()

                    @pl.when(jnp.logical_not(own))
                    def _():
                        remote(src, dst, ys_sem.at[kind, i], got, {'cp': to_row, 'tp': col * CORES + row // half_cp}).start()

    def share(b):
        for rr in range(half_cp):
            r = core * half_cp + rr
            some = pl.ds(0, batch_units)
            pltpu.make_async_copy(kv_all.at[r, some], kv_all.at[r, some], ykv_sem.at[rr, b]).wait()
            for o, c, h in BATCHES[b]:
                unit = unit_of(o, c, h)
                remote(kv_all.at[r, unit], kv_all.at[r, unit], ks_sem, kr_sem.at[rr, b], sibling).start()

    part_rows = wo_rows // n_half

    def wo_part(t, h):
        return wo_all.at[pl.ds(pl.multiple_of(t * wo_rows + h * part_rows, part_rows), part_rows)]

    def column(o, other=0):
        return lax.rem(col + o, x_devs) * CORES + (1 - core if other else core)

    def wo_direct(d, h):
        return remote(wo_part(tp, h), wo_part(tp, h), ws_sem.at[d - 1, h], wr_sem.at[x_devs - d - 1, h], beside(d))

    def wo_from(o, h):
        t = column(o)
        return remote(wo_part(t, h), wo_part(t, h), ws_sem.at[o - 1, h], wr_sem.at[o - 1, h], sibling)

    def wo_onward(o, h):
        t = column(o)
        return remote(wo_part(t, h), wo_part(t, h), ws_sem.at[1, h], wr_sem.at[1, h], beside(ONWARD[(o, h)]))

    def wo_handed(o, h, other=0):
        t = column(o, other)
        return remote(wo_part(t, h), wo_part(t, h), wfs_sem.at[o, h], wfr_sem.at[o, h], sibling)

    def wo_start():
        for d, h in SEND_ORDER:
            wo_direct(d, h).start()
        for h in range(n_half):
            wo_handed(0, h).start()

    for load in loads:
        load.wait()
    for b in range(len(BATCHES)):
        with jax.named_scope('a_xwait'):
            for o, c, h in BATCHES[b]:
                if c == 0 and o:
                    (onward(h) if o == 2 else direct(x_devs - o, h)).wait_recv()
                    if (o, h) in ONWARD:
                        onward(h).start()
                    handed(o, h).start()
            for o, c, h in BATCHES[b]:
                if c == 1:
                    handed(o, h).wait_recv()

        with jax.named_scope('a_qkv'):
            @pl.loop(0, 3)
            def _(n):
                y = jnp.dot(xg[b].reshape(batch_units * half_rows, hidden), w_in[n], preferred_element_type=f32).astype(bf16)
                for i in range(n_heads_loc):
                    for u in range(batch_units):
                        stage[b, i, u, n] = y[u * half_rows:(u + 1) * half_rows, i * LANES:(i + 1) * LANES]

        with jax.named_scope('a_exch'):
            exchange(b)
            if b == len(BATCHES) - 1:
                wo_start()
        with jax.named_scope('a_share'):
            if b:
                share(b - 1)
    with jax.named_scope('a_share_last'):
        share(len(BATCHES) - 1)

    with jax.named_scope('a_kvwait'):
        for rr in range(half_cp):
            for b in range(len(BATCHES)):
                some = pl.ds(0, batch_units)
                pltpu.make_async_copy(q_all.at[rr, some], q_all.at[rr, some], yq_sem.at[rr, b]).wait()
                other = (1 - core) * half_cp + rr
                remote(kv_all.at[other, some], kv_all.at[other, some], ks_sem, kr_sem.at[rr, b], sibling).wait_recv()

    scale = LANES ** -0.5 * math.log2(math.e)
    sub_units = half_units // 2
    sub_rows = sub_units * half_rows
    repeat = half_units * half_rows // LANES
    head = col * cp_devs + row

    def scores(q, keys):
        return lax.dot_general(q, keys, (((1,), (1,)), ((), ())), preferred_element_type=f32) * scale

    def lane_sums(p):
        total = p[:, :LANES]
        for i in range(1, p.shape[1] // LANES):
            total += p[:, i * LANES:(i + 1) * LANES]
        return total

    @pl.loop(0, 2 * half_cp)
    def _(piece):
        rr, late = piece // 2, lax.rem(piece, 2)
        block = core * half_cp + rr
        place = jnp.where(late == 0, block, 2 * cp_devs - 1 - block)
        with jax.named_scope('a_flash'):
            for sub in range(2):
                q = q_all[rr, pl.ds(late * half_units + sub * sub_units, sub_units)].reshape(sub_rows, LANES)
                near = (sub + 1) * sub_units
                keys = kv_all[block, pl.ds(late * half_units, near), 0].reshape(near * half_rows, LANES)
                vals = kv_all[block, pl.ds(late * half_units, near), 1].reshape(near * half_rows, LANES)
                s = scores(q, keys)
                q_at = sub * sub_rows + lax.broadcasted_iota(jnp.int32, s.shape, 0)
                s = jnp.where(lax.broadcasted_iota(jnp.int32, s.shape, 1) <= q_at, s, -1e30)
                m = jnp.broadcast_to(jnp.max(s, axis=1, keepdims=True), (sub_rows, LANES))
                p = jnp.exp2(s - jnp.concatenate([m] * (s.shape[1] // LANES), axis=1))
                m_run[...] = m
                l_run[...] = lane_sums(p)
                acc[...] = jnp.dot(p.astype(bf16), vals, preferred_element_type=f32)

                @pl.loop(0, place)
                def _(kp):
                    k_block = jnp.where(kp < cp_devs, kp, 2 * cp_devs - 1 - kp)
                    k_first = jnp.where(kp < cp_devs, 0, half_units)
                    keys = kv_all[k_block, pl.ds(k_first, half_units), 0].reshape(half_units * half_rows, LANES)
                    vals = kv_all[k_block, pl.ds(k_first, half_units), 1].reshape(half_units * half_rows, LANES)
                    s = scores(q_all[rr, pl.ds(late * half_units + sub * sub_units, sub_units)].reshape(sub_rows, LANES), keys)
                    before = m_run[...]
                    m = jnp.maximum(before, jnp.max(s, axis=1, keepdims=True))
                    p = jnp.exp2(s - jnp.concatenate([m] * repeat, axis=1))
                    fade = jnp.exp2(before - m)
                    m_run[...] = m
                    l_run[...] = fade * l_run[...] + lane_sums(p)
                    acc[...] = fade * acc[...] + jnp.dot(p.astype(bf16), vals, preferred_element_type=f32)

                o = acc[...] / jnp.sum(l_run[...], axis=1, keepdims=True)
                o_st[rr, pl.ds(late * half_units + sub * sub_units, sub_units)] = o.astype(bf16).reshape(sub_units, half_rows, LANES)

        for t in range(tp_devs // 2):
            to_tp = late * (tp_devs // 2) + t
            src = o_st.at[rr, pl.ds(to_tp * n_half, n_half)]
            own = jnp.logical_and(block == row, to_tp == tp)

            @pl.when(own)
            def _():
                pltpu.make_async_copy(src, og.at[head], or_sem).start()

            @pl.when(jnp.logical_not(own))
            def _():
                remote(src, og.at[head], os_sem, or_sem, {'cp': block, 'tp': to_tp}).start()

        @pl.when(piece == 0)
        def _():
            for o, h in ONWARD:
                wo_from(o, h).wait_recv()
                wo_onward(o, h).start()
                wo_handed(o, h).start()

        @pl.when(piece == 2)
        def _():
            for o, h in ((3, 1), (1, 0)):
                wo_from(o, h).wait_recv()
                wo_handed(o, h).start()

    with jax.named_scope('a_wo2'):
        for h in range(n_half):
            wo_from(2, h).wait_recv()
            wo_handed(2, h).start()
    with jax.named_scope('a_owait'):
        pltpu.make_async_copy(og, og, or_sem).wait()
    for n in range(og.shape[0]):
        o_rows[:, n * LANES:(n + 1) * LANES] = og[n].reshape(n_half * half_rows, LANES)
    with jax.named_scope('a_wowait'):
        for o in range(x_devs):
            for h in range(n_half):
                wo_handed(o, h, 1).wait_recv()

    sub = hidden // LANES
    step = 2 * LANES
    rows = n_half * half_rows

    with jax.named_scope('a_proj'):
        @pl.loop(0, hidden // step)
        def _(j):
            cols = pl.ds(pl.multiple_of(j * step, step), step)
            h = jnp.dot(o_rows[...], wo_all[:, cols], preferred_element_type=f32) + hid_ref[:, :, cols].reshape(rows, step).astype(f32)
            for i in range(step // LANES):
                wide[pl.ds(j * (step // LANES) + i, rows, stride=sub), :] = h[:, i * LANES:(i + 1) * LANES]

    with jax.named_scope('a_rows'):
        @pl.loop(0, rows // 8)
        def _(t):
            for i in range(8):
                h_ref[t * 8 + i] = wide[pl.ds(pl.multiple_of((t * 8 + i) * sub, sub), sub), :].astype(bf16)

    with jax.named_scope('a_drain'):
        for d, h in SEND_ORDER:
            direct(d, h).wait_send()
        for o in range(x_devs):
            for h in range(n_half):
                handed(o, h).wait_send()
                wo_handed(o, h).wait_send()
        for d, h in SEND_ORDER:
            wo_direct(d, h).wait_send()
        for o, h in ONWARD:
            onward(h).wait_send()
            wo_onward(o, h).wait_send()
        for i in range(n_heads_loc):
            @pl.when(core * n_heads_loc + i != row)
            def _():
                remote(q_all.at[0], q_all.at[0], ys_sem.at[0, i], yq_sem.at[0, 0], sibling).wait_send()
                remote(kv_all.at[0], kv_all.at[0], ys_sem.at[1, i], ykv_sem.at[0, 0], sibling).wait_send()
        every = kv_all.at[pl.ds(0, half_cp)]
        remote(every, every, ks_sem, kr_sem.at[0, 0], sibling).wait_send()
        own_row = row // half_cp == core

        @pl.when(own_row)
        def _():
            most = og.at[pl.ds(0, og.shape[0] - 1)]
            remote(most, most, os_sem, or_sem, sibling).wait_send()

        @pl.when(jnp.logical_not(own_row))
        def _():
            remote(og, og, os_sem, or_sem, sibling).wait_send()


def attention_residual(hidden_in, w_query, w_key, w_value, w_out, cp_devs, tp_devs):
    tok_dev, hidden = hidden_in.shape
    heads_loc, head_dim = w_query.shape[1:]
    if w_key.shape != w_query.shape or head_dim != LANES or tp_devs != RING * CORES or heads_loc * CORES != cp_devs:
        raise ValueError('unexpected sizes')
    n_half = 2
    half_rows = tok_dev // n_half
    units = tp_devs * n_half
    n_heads = heads_loc * tp_devs
    batches, batch_units = len(BATCHES), len(BATCHES[0])
    half_cp = cp_devs // 2
    sub = hidden // LANES
    sub_rows = units // 4 * half_rows
    bf16, f32 = jnp.bfloat16, jnp.float32
    dma = pltpu.SemaphoreType.DMA
    flat = [w.reshape(hidden, heads_loc * head_dim) for w in (w_query, w_key, w_value)]
    return pl.pallas_call(
        functools.partial(attention_kernel, cp_devs, tp_devs),
        out_shape=jax.ShapeDtypeStruct((tok_dev, sub, LANES), bf16),
        in_specs=[pl.BlockSpec(memory_space=pltpu.VMEM)] + [pl.BlockSpec(memory_space=pl.ANY)] * 4,
        out_specs=pl.BlockSpec(memory_space=pltpu.VMEM),
        scratch_shapes=[
            pltpu.VMEM((3, hidden, heads_loc * head_dim), bf16),
            pltpu.VMEM((batches, batch_units, half_rows, hidden), bf16),
            pltpu.VMEM((batches, heads_loc, batch_units, 3, half_rows, LANES), bf16),
            pltpu.VMEM((half_cp, units, half_rows, LANES), bf16),
            pltpu.VMEM((cp_devs, units, 2, half_rows, LANES), bf16),
            pltpu.VMEM((half_cp, units, half_rows, LANES), bf16),
            pltpu.VMEM((n_heads, n_half, half_rows, LANES), bf16),
            pltpu.VMEM((tok_dev, hidden), bf16),
            pltpu.VMEM((n_heads * head_dim, hidden), bf16),
            pltpu.VMEM((tok_dev * sub, LANES), f32),
            pltpu.VMEM((sub_rows, LANES), f32),
            pltpu.VMEM((sub_rows, LANES), f32),
            pltpu.VMEM((sub_rows, LANES), f32),
            dma((RING - 1, n_half)), dma((RING - 1, n_half)), dma((RING, n_half)), dma((RING, n_half)),
            dma((2, heads_loc)), dma((half_cp, batches)), dma((half_cp, batches)), dma, dma((half_cp, batches)),
            dma((RING - 1, n_half)), dma((RING - 1, n_half)), dma((RING, n_half)), dma((RING, n_half)), dma, dma, dma((4,)),
        ],
        compiler_params=pltpu.CompilerParams(collective_id=1, has_side_effects=True, vmem_limit_bytes=67043328),
        cost_estimate=pl.CostEstimate(flops=12 * 10 ** 9, bytes_accessed=16 * 10 ** 6, transcendentals=10 ** 7),
        name='attention_exchange',
    )(hidden_in.reshape(n_half, half_rows, hidden), *flat, w_out.reshape(heads_loc * head_dim, hidden))


from jax.sharding import PartitionSpec as P


def solution(mesh):
    cp_devs, tp_devs = mesh.shape['cp'], mesh.shape['tp']
    row_spec = P(('dp', 'cp', 'tp'), None)
    head_spec = P(None, 'tp', None)
    expert_spec = P(('cp', 'tp'), None, None)

    def device_step(hidden_in, w_query, w_key, w_value, w_out, expert_idx, gate_vals, w_gate, w_up, w_down):
        h_tiles = attention_residual(hidden_in, w_query, w_key, w_value, w_out, cp_devs, tp_devs)
        return moe(h_tiles, expert_idx, gate_vals, w_gate, w_up, w_down, cp_devs, tp_devs)

    return jax.shard_map(device_step, mesh=mesh, in_specs=(row_spec, head_spec, head_spec, head_spec, P('tp', None, None), row_spec, row_spec, expert_spec, expert_spec, expert_spec), out_specs=row_spec, check_vma=False)
```

time: 273 us -> 200 us (0.73)
  Pallas kernels: 257 us -> 188 us
    pallas_call x1, Pallas kernels: 130 us -> 89.8 us  [attention_residual(): pl.pallas_call(functools.partial(attention_kernel, cp_devs, tp_devs), out...]
    pallas_call x1, Pallas kernels: 128 us -> 98.7 us  [moe(): pl.pallas_call(functools.partial(moe_kernel, cp_devs, tp_devs, chunks), o...]
    another operation x3 -> x0, local copies, waits for them, and re-layouts: 4.18 us -> none  [attention_residual(): jnp.stack([w.reshape(hidden, heads_loc * head_dim) for w in (w_query, w_k...]
where the time goes in v2:
time: 200 us; the launch traced here: 199 us
  Pallas kernels  188 us (94%)
  local copies, waits for them, and re-layouts  7.67 us (4%)
  other arithmetic  3.09 us (2%)
    pallas_call x1, Pallas kernels, moe(): pl.pallas_call(functools.partial(moe_kernel, cp_devs, tp_devs, chunks), o...  98.7 us
    pallas_call x1, Pallas kernels, attention_residual(): pl.pallas_call(functools.partial(attention_kernel, cp_devs, tp_devs), out...  89.8 us
    unnamed x2, local copies, waits for them, and re-layouts  4.44 us

profile of v2, /device:TPU:97, one launch (start us, length us, event | category | flops | bytes accessed | tf_op | source)
XLA Modules:
  0.0 199.4 jit_solution(18315068440848587364)
XLA Ops:
  0.0 0.7 add_select_fusion.3
  0.7 0.2 convolution_convert_fusion
  0.9 0.1 select_reduce_fusion.1
  1.0 1.0 select_reduce_fusion
  2.0 1.3 fusion.8.pos_ref
  3.3 2.4 %copy.20 = bf16[256,8,2,128]{3,1,2,0:T(8,128)(2,1)} copy(bf16[256,8,2,128]{3,2,1,0:T(2,128)(2,1)} %bitcast.17) | data formatting | bytes 2097152
  5.6 3.2 %copy_bitcast_fusion = (bf16[2048,256]{1,0:T(8,128)(2,1)}, bf16[2048,256]{1,0:T(8,128)(2,1)}) fusion(bf16[256,8,2,128]{3,2,1,0:T(2,128)(2,1)} %bitcast.19, bf16[256,8,2,128]{3,2,1,0:T(2,128)(2,1)} %bitcast.20), kind=kLoop, calls=%fused_computation.1 | loop fusion | bytes 4194304 | tf_op jit(solution)/shard_map/reshape | solution.py:565
  8.8 89.8 %attention_exchange.1.h_ref = bf16[192,16,128]{2,1,0:T(8,128)(2,1)} custom-call(bf16[2,96,2048]{2,1,0:T(8,128)(2,1)} %bitcast.23, bf16[2048,256]{1,0:T(8,128)(2,1)} %bitcast.18, bf16[2048,256]{1,0:T(8,128)(2,1)} %get-tuple-element.6.wk_ref, bf16[2048,256]{1,0:T(8,128)(2,1)} %get-tuple-element.5.wv_ref, bf16[256,2048]{1,0:T(8,128)(2,1)} %bitcast.22), custom_call_target="tpu_custom_call" | custom-call | flops 12000000000 | bytes 16000000 | tf_op jit(solution)/shard_map/attention_exchange/pallas_call | solution.py:566
  98.6 98.7 %moe_exchange.1 = bf16[192,2048]{1,0:T(8,128)(2,1)} custom-call(s32[18,32]{1,0:T(8,128)} %bitcast.21, s32[6,192]{1,0:T(8,128)} %fusion.8.pos_ref, f32[6,192]{1,0:T(8,128)} %bitcast.24, bf16[192,16,128]{2,1,0:T(8,128)(2,1)} %attention_exchange.1.h_ref, bf16[2,2048,1408]{2,1,0:T(8,128)(2,1)} %wg_ref.1, bf16[2,2048,1408]{2,1,0:T(8,128)(2,1)} %wu_ref.1, ...), custom_call_target="tpu_custom_call" | custom-call | flops 19931332608 | bytes 34603008 | tf_op jit(solution)/shard_map/moe_exchange/pallas_call | solution.py:207
  197.3 2.1 %copy.22 = bf16[192,2048]{1,0:T(8,128)(2,1)} copy(bf16[192,2048]{1,0:T(8,128)(2,1)} %moe_exchange.1) | data formatting | bytes 1572864
  (1 shorter events, 0.0 us)

commit v3 on v2

--- a/solution.py
+++ b/solution.py
@@ -70,7 +70,7 @@
     def fill(dev, carry):
         for c in range(chunks):
             for s in range(slots):
-                send[c, dev, s] = h_ref[src_ref[c * slots + s, dev]]
+                send[c, dev, s] = h_ref[src_ref[dev, c * slots + s]]
         return carry
 
     with jax.named_scope('m_fill'):
@@ -175,33 +175,45 @@
             y_ref[:, q * LANES:(q + 1) * LANES] = wide[pl.ds(q, tok_dev, stride=sub), :].astype(jnp.bfloat16)
 
 
-def routing_tables(expert_idx, local_exp, n_dev, chunks):
-    tok_dev, top_k = expert_idx.shape
+def routing_tables(idx_ref, src_ref, pos_ref, n_dev, local_exp, chunks):
+    top_k, tok_dev = idx_ref.shape
     per_dev = tok_dev * top_k // (n_dev * local_exp)
     slots = per_dev // chunks
-    dev = expert_idx // local_exp
-    devs = jnp.arange(n_dev)
-    member = jnp.any(dev[:, :, None] == devs[None, None, :], axis=1)
-    before = (jnp.arange(tok_dev)[:, None] > jnp.arange(tok_dev)[None, :]).astype(jnp.bfloat16)
-    slot_all = jnp.dot(before, member.astype(jnp.bfloat16), preferred_element_type=jnp.float32).astype(jnp.int32)
-    slot = jnp.sum(jnp.where(dev[:, :, None] == devs[None, None, :], slot_all[:, None, :], 0), axis=2)
-    here = member[:, :, None] & (slot_all[:, :, None] == jnp.arange(per_dev)[None, None, :])
-    src = jnp.sum(jnp.where(here, jnp.arange(tok_dev, dtype=jnp.int32)[:, None, None], 0), axis=0)
-    pos = (((slot // slots) * n_dev + dev) * local_exp + expert_idx % local_exp) * slots + slot % slots
-    return src.T, pos.T
-
-
-def moe(h_tiles, expert_idx, gate_vals, w_gate, w_up, w_down, cp_devs, tp_devs, chunks=3):
+    shape = (n_dev, tok_dev)
+    devs = lax.broadcasted_iota(jnp.int32, shape, 0)
+    chosen = [idx_ref[k:k + 1, :] for k in range(top_k)]
+    target = [e >> (local_exp.bit_length() - 1) for e in chosen]
+    member = target[0] == devs
+    for d in target[1:]:
+        member = jnp.logical_or(member, d == devs)
+    pair = (tok_dev, tok_dev)
+    before = jnp.where(lax.broadcasted_iota(jnp.int32, pair, 0) < lax.broadcasted_iota(jnp.int32, pair, 1), 1.0, 0.0).astype(jnp.bfloat16)
+    slot_all = jnp.dot(jnp.where(member, 1.0, 0.0).astype(jnp.bfloat16), before, preferred_element_type=jnp.float32)
+    for k in range(top_k):
+        slot = jnp.sum(jnp.where(target[k] == devs, slot_all, 0.0), axis=0, keepdims=True).astype(jnp.int32)
+        chunk = jnp.zeros_like(slot)
+        for c in range(1, chunks):
+            chunk += jnp.where(slot >= c * slots, 1, 0)
+        pos_ref[k:k + 1, :] = (((chunk * n_dev + target[k]) * local_exp + chosen[k] - target[k] * local_exp) * slots) + slot - chunk * slots
+    token = lax.broadcasted_iota(jnp.int32, shape, 1).astype(jnp.float32)
+    lane = lax.broadcasted_iota(jnp.int32, src_ref.shape, 1)
+    table = jnp.zeros(src_ref.shape, jnp.float32)
+    for s in range(per_dev):
+        here = jnp.sum(jnp.where(jnp.logical_and(member, slot_all == s), token, 0.0), axis=1, keepdims=True)
+        table = jnp.where(lane == s, here, table)
+    src_ref[...] = table.astype(jnp.int32)
+
+
+def moe(h_tiles, src, pos, gate_vals, w_gate, w_up, w_down, cp_devs, tp_devs, chunks):
     tok_dev, sub, _ = h_tiles.shape
     hidden = sub * LANES
     local_exp, _, ffn = w_gate.shape
-    top_k = expert_idx.shape[1]
+    top_k = gate_vals.shape[1]
     n_dev = cp_devs * tp_devs
     slots = tok_dev * top_k // (n_dev * local_exp) // chunks
     rows = n_dev * slots
     gu_tiles, dn_cols = ffn // LANES, 2 * LANES
     dn_tiles = hidden // dn_cols
-    src, pos = routing_tables(expert_idx, local_exp, n_dev, chunks)
     bf16, f32 = jnp.bfloat16, jnp.float32
     flops = 6 * chunks * rows * local_exp * hidden * ffn
     out = pl.pallas_call(
@@ -238,13 +250,14 @@
            ((3, 0, 0), (3, 1, 0), (1, 0, 1), (1, 1, 1)),
            ((3, 0, 1), (3, 1, 1), (1, 0, 0), (1, 1, 0)),
            ((2, 0, 0), (2, 0, 1), (2, 1, 0), (2, 1, 1)))
+STEPS = ((0, 0, 1), (1, 0, 1), (2, 0, 1), (3, 0, 2), (3, 1, 2))
 SEND_ORDER = ((1, 0), (3, 1), (1, 1), (3, 0))
 ONWARD = {(3, 0): 1, (1, 1): 3}
 
 
-def attention_kernel(cp_devs, tp_devs, hid_ref, wq_ref, wk_ref, wv_ref, wo_ref, h_ref,
-                     w_in, xg, stage, q_all, kv_all, o_st, og, o_rows, wo_all, wide, acc, m_run, l_run,
-                     xs_sem, xr_sem, fs_sem, fr_sem, ys_sem, yq_sem, ykv_sem, ks_sem, kr_sem, ws_sem, wr_sem, wfs_sem, wfr_sem, os_sem, or_sem, in_sem):
+def attention_kernel(cp_devs, tp_devs, local_exp, chunks, hid_ref, wq_ref, wk_ref, wv_ref, wo_ref, idx_ref, h_ref, src_ref, pos_ref,
+                     w_raw, w_in, xg, x_last, stage, stage_last, q_all, kv_all, o_st, og, o_rows, wo_all, wide, acc, m_run, l_run,
+                     xs_sem, xr_sem, fs_sem, fr_sem, ons_sem, onr_sem, fls_sem, flr_sem, ys_sem, yq_sem, ykv_sem, ks_sem, kr_sem, ws_sem, wr_sem, wfs_sem, wfr_sem, wos_sem, wor_sem, vs_sem, vr_sem, us_sem, ur_sem, hs_sem, hr_sem, os_sem, or_sem, in_sem):
     row, tp = lax.axis_index('cp'), lax.axis_index('tp')
     col, core = tp // CORES, lax.rem(tp, CORES)
     x_devs = tp_devs // CORES
@@ -274,7 +287,7 @@
         return carry
 
     lax.fori_loop(1, n_dev, greet, 0)
-    loads = [pltpu.make_async_copy(ref, w_in.at[n], in_sem.at[n]) for n, ref in enumerate((wq_ref, wk_ref, wv_ref))]
+    loads = [pltpu.make_async_copy(ref, w_raw.at[n], in_sem.at[n]) for n, ref in enumerate((wq_ref, wk_ref, wv_ref))]
     loads.append(pltpu.make_async_copy(wo_ref, wo_all.at[pl.ds(pl.multiple_of(tp * wo_rows, wo_rows), wo_rows)], in_sem.at[3]))
     for load in loads:
         load.start()
@@ -290,11 +303,16 @@
         b, u = where[(o, 0, h)]
         return remote(hid_ref.at[h], xg.at[b, u], xs_sem.at[d - 1, h], xr_sem.at[o - 1, h], beside(d))
 
-    def onward(h):
+    last_rows = x_last.shape[2]
+
+    def onward(h, part):
         o = 3 if h == 0 else 1
         b, u = where[(o, 0, h)]
-        b2, u2 = where[(2, 0, h)]
-        return remote(xg.at[b, u], xg.at[b2, u2], xs_sem.at[1, h], xr_sem.at[1, h], beside(ONWARD[(o, h)]))
+        return remote(xg.at[b, u, pl.ds(part * last_rows, last_rows)], x_last.at[part, where[(2, 0, h)][1]], ons_sem.at[h, part], onr_sem.at[h, part],
+                      beside(ONWARD[(o, h)]))
+
+    def handed_last(h, part):
+        return remote(x_last.at[part, where[(2, 0, h)][1]], x_last.at[part, where[(2, 1, h)][1]], fls_sem.at[h, part], flr_sem.at[h, part], sibling)
 
     def handed(o, h):
         b, u = where[(o, 0, h)]
@@ -310,15 +328,22 @@
     def unit_of(o, c, h):
         return (lax.rem(col + o, x_devs) * CORES + lax.rem(core + c, CORES)) * n_half + h
 
-    def exchange(b):
+    def rows_of(step):
+        b, part, parts = STEPS[step]
+        return BATCHES[b], pl.ds(part * (half_rows // parts), half_rows // parts)
+
+    def exchange(step):
+        b, part, parts = STEPS[step]
+        batch, some = rows_of(step)
+        done = stage.at[b] if parts == 1 else stage_last.at[part]
         for i in range(n_heads_loc):
             to_row = core * n_heads_loc + i
             own = to_row == row
-            for u, (o, c, h) in enumerate(BATCHES[b]):
+            for u, (o, c, h) in enumerate(batch):
                 unit = unit_of(o, c, h)
-                for kind, src, dst, sem in ((0, stage.at[b, i, u, 0], q_all.at[lax.rem(row, half_cp), unit], yq_sem),
-                                            (1, stage.at[b, i, u, pl.ds(1, 2)], kv_all.at[row, unit], ykv_sem)):
-                    got = sem.at[lax.rem(row, half_cp), b]
+                for kind, src, dst, sem in ((0, done.at[i, u, 0], q_all.at[lax.rem(row, half_cp), unit, some], yq_sem),
+                                            (1, done.at[i, u, pl.ds(1, 2)], kv_all.at[row, unit, :, some], ykv_sem)):
+                    got = sem.at[lax.rem(row, half_cp), step]
 
                     @pl.when(own)
                     def _():
@@ -328,19 +353,27 @@
                     def _():
                         remote(src, dst, ys_sem.at[kind, i], got, {'cp': to_row, 'tp': col * CORES + row // half_cp}).start()
 
-    def share(b):
+    def share(step):
+        batch, some = rows_of(step)
         for rr in range(half_cp):
             r = core * half_cp + rr
-            some = pl.ds(0, batch_units)
-            pltpu.make_async_copy(kv_all.at[r, some], kv_all.at[r, some], ykv_sem.at[rr, b]).wait()
-            for o, c, h in BATCHES[b]:
-                unit = unit_of(o, c, h)
-                remote(kv_all.at[r, unit], kv_all.at[r, unit], ks_sem, kr_sem.at[rr, b], sibling).start()
-
-    part_rows = wo_rows // n_half
+            every = kv_all.at[r, pl.ds(0, batch_units), :, some]
+            pltpu.make_async_copy(every, every, ykv_sem.at[rr, step]).wait()
+            for o, c, h in batch:
+                one = kv_all.at[r, unit_of(o, c, h), :, some]
+                remote(one, one, ks_sem, kr_sem.at[rr, step], sibling).start()
+
+    ring_rows = wo_rows // (2 * n_half)
+    share_rows = wo_rows // (2 * cp_devs)
+
+    def wo_rows_at(t, first, n):
+        return wo_all.at[pl.ds(pl.multiple_of(t * wo_rows + first, n), n)]
 
     def wo_part(t, h):
-        return wo_all.at[pl.ds(pl.multiple_of(t * wo_rows + h * part_rows, part_rows), part_rows)]
+        return wo_rows_at(t, h * ring_rows, ring_rows)
+
+    def wo_share(t):
+        return wo_rows_at(t, wo_rows // 2 + row * share_rows, share_rows)
 
     def column(o, other=0):
         return lax.rem(col + o, x_devs) * CORES + (1 - core if other else core)
@@ -354,57 +387,105 @@
 
     def wo_onward(o, h):
         t = column(o)
-        return remote(wo_part(t, h), wo_part(t, h), ws_sem.at[1, h], wr_sem.at[1, h], beside(ONWARD[(o, h)]))
+        return remote(wo_part(t, h), wo_part(t, h), wos_sem.at[h], wor_sem.at[h], beside(ONWARD[(o, h)]))
 
     def wo_handed(o, h, other=0):
         t = column(o, other)
         return remote(wo_part(t, h), wo_part(t, h), wfs_sem.at[o, h], wfr_sem.at[o, h], sibling)
 
+    def wo_across(d):
+        return remote(wo_share(tp), wo_share(tp), vs_sem.at[d - 1], vr_sem.at[x_devs - d - 1], beside(d))
+
+    def wo_along(o, e):
+        t = column(o)
+        return remote(wo_share(t), wo_share(t), us_sem, ur_sem, {'cp': lax.rem(row + e, cp_devs), 'tp': tp})
+
+    def wo_rest_handed(o, other=0):
+        part = wo_rows_at(column(o, other), wo_rows // 2, wo_rows // 2)
+        return remote(part, part, hs_sem.at[o], hr_sem.at[o], sibling)
+
     def wo_start():
+        for d in range(1, x_devs):
+            wo_across(d).start()
         for d, h in SEND_ORDER:
             wo_direct(d, h).start()
         for h in range(n_half):
             wo_handed(0, h).start()
+        wo_rest_handed(0).start()
+
+    def wo_spread():
+        for o in range(1, x_devs):
+            t = column(o)
+            remote(wo_share(t), wo_share(t), vs_sem.at[o - 1], vr_sem.at[o - 1], sibling).wait_recv()
+        for e in (2, 1, 3):
+            for o in range(1, x_devs):
+                wo_along(o, e).start()
+
+    all_along = wo_all.at[pl.ds(0, (x_devs - 1) * (cp_devs - 1) * share_rows)]
 
     for load in loads:
         load.wait()
-    for b in range(len(BATCHES)):
+    with jax.named_scope('a_weights'):
+        some_rows = 2 * LANES
+
+        @pl.loop(0, hidden // some_rows)
+        def _(i):
+            at = pl.ds(pl.multiple_of(i * some_rows, some_rows), some_rows)
+            for n in range(3):
+                w_in[n, at, :] = w_raw[n, at].reshape(some_rows, w_in.shape[2])
+
+    for step, (b, part, parts) in enumerate(STEPS):
         with jax.named_scope('a_xwait'):
             for o, c, h in BATCHES[b]:
                 if c == 0 and o:
-                    (onward(h) if o == 2 else direct(x_devs - o, h)).wait_recv()
+                    (onward(h, part) if o == 2 else direct(x_devs - o, h)).wait_recv()
                     if (o, h) in ONWARD:
-                        onward(h).start()
-                    handed(o, h).start()
+                        onward(h, 0).start()
+                        onward(h, 1).start()
+                    (handed_last(h, part) if o == 2 else handed(o, h)).start()
             for o, c, h in BATCHES[b]:
                 if c == 1:
-                    handed(o, h).wait_recv()
+                    (handed_last(h, part) if o == 2 else handed(o, h)).wait_recv()
 
         with jax.named_scope('a_qkv'):
+            n_rows = half_rows // parts
+
             @pl.loop(0, 3)
             def _(n):
-                y = jnp.dot(xg[b].reshape(batch_units * half_rows, hidden), w_in[n], preferred_element_type=f32).astype(bf16)
+                x = xg[b] if parts == 1 else x_last[part]
+                y = jnp.dot(x.reshape(batch_units * n_rows, hidden), w_in[n], preferred_element_type=f32).astype(bf16)
                 for i in range(n_heads_loc):
                     for u in range(batch_units):
-                        stage[b, i, u, n] = y[u * half_rows:(u + 1) * half_rows, i * LANES:(i + 1) * LANES]
+                        val = y[u * n_rows:(u + 1) * n_rows, i * LANES:(i + 1) * LANES]
+                        if parts == 1:
+                            stage[b, i, u, n] = val
+                        else:
+                            stage_last[part, i, u, n] = val
 
         with jax.named_scope('a_exch'):
-            exchange(b)
-            if b == len(BATCHES) - 1:
+            exchange(step)
+            if step == 1:
                 wo_start()
         with jax.named_scope('a_share'):
-            if b:
-                share(b - 1)
+            if step in (1, 2):
+                share(step - 1)
+        if step == 0:
+            with jax.named_scope('a_tables'):
+                routing_tables(idx_ref, src_ref, pos_ref, n_dev, local_exp, chunks)
     with jax.named_scope('a_share_last'):
-        share(len(BATCHES) - 1)
+        for step in range(2, len(STEPS)):
+            share(step)
+    with jax.named_scope('a_wospread'):
+        wo_spread()
 
     with jax.named_scope('a_kvwait'):
         for rr in range(half_cp):
-            for b in range(len(BATCHES)):
-                some = pl.ds(0, batch_units)
-                pltpu.make_async_copy(q_all.at[rr, some], q_all.at[rr, some], yq_sem.at[rr, b]).wait()
-                other = (1 - core) * half_cp + rr
-                remote(kv_all.at[other, some], kv_all.at[other, some], ks_sem, kr_sem.at[rr, b], sibling).wait_recv()
+            for step in range(len(STEPS)):
+                _, some = rows_of(step)
+                got = q_all.at[rr, pl.ds(0, batch_units), some]
+                pltpu.make_async_copy(got, got, yq_sem.at[rr, step]).wait()
+                got = kv_all.at[(1 - core) * half_cp + rr, pl.ds(0, batch_units), :, some]
+                remote(got, got, ks_sem, kr_sem.at[rr, step], sibling).wait_recv()
 
     scale = LANES ** -0.5 * math.log2(math.e)
     sub_units = half_units // 2
@@ -427,36 +508,40 @@
         block = core * half_cp + rr
         place = jnp.where(late == 0, block, 2 * cp_devs - 1 - block)
         with jax.named_scope('a_flash'):
+            def queries(sub):
+                return q_all[rr, pl.ds(late * half_units + sub * sub_units, sub_units)].reshape(sub_rows, LANES)
+
             for sub in range(2):
-                q = q_all[rr, pl.ds(late * half_units + sub * sub_units, sub_units)].reshape(sub_rows, LANES)
                 near = (sub + 1) * sub_units
                 keys = kv_all[block, pl.ds(late * half_units, near), 0].reshape(near * half_rows, LANES)
                 vals = kv_all[block, pl.ds(late * half_units, near), 1].reshape(near * half_rows, LANES)
-                s = scores(q, keys)
+                s = scores(queries(sub), keys)
                 q_at = sub * sub_rows + lax.broadcasted_iota(jnp.int32, s.shape, 0)
                 s = jnp.where(lax.broadcasted_iota(jnp.int32, s.shape, 1) <= q_at, s, -1e30)
                 m = jnp.broadcast_to(jnp.max(s, axis=1, keepdims=True), (sub_rows, LANES))
                 p = jnp.exp2(s - jnp.concatenate([m] * (s.shape[1] // LANES), axis=1))
-                m_run[...] = m
-                l_run[...] = lane_sums(p)
-                acc[...] = jnp.dot(p.astype(bf16), vals, preferred_element_type=f32)
-
-                @pl.loop(0, place)
-                def _(kp):
-                    k_block = jnp.where(kp < cp_devs, kp, 2 * cp_devs - 1 - kp)
-                    k_first = jnp.where(kp < cp_devs, 0, half_units)
-                    keys = kv_all[k_block, pl.ds(k_first, half_units), 0].reshape(half_units * half_rows, LANES)
-                    vals = kv_all[k_block, pl.ds(k_first, half_units), 1].reshape(half_units * half_rows, LANES)
-                    s = scores(q_all[rr, pl.ds(late * half_units + sub * sub_units, sub_units)].reshape(sub_rows, LANES), keys)
-                    before = m_run[...]
+                m_run[sub] = m
+                l_run[sub] = lane_sums(p)
+                acc[sub] = jnp.dot(p.astype(bf16), vals, preferred_element_type=f32)
+
+            @pl.loop(0, place)
+            def _(kp):
+                k_block = jnp.where(kp < cp_devs, kp, 2 * cp_devs - 1 - kp)
+                k_first = jnp.where(kp < cp_devs, 0, half_units)
+                keys = kv_all[k_block, pl.ds(k_first, half_units), 0].reshape(half_units * half_rows, LANES)
+                vals = kv_all[k_block, pl.ds(k_first, half_units), 1].reshape(half_units * half_rows, LANES)
+                both = [scores(queries(sub), keys) for sub in range(2)]
+                for sub, s in enumerate(both):
+                    before = m_run[sub]
                     m = jnp.maximum(before, jnp.max(s, axis=1, keepdims=True))
                     p = jnp.exp2(s - jnp.concatenate([m] * repeat, axis=1))
                     fade = jnp.exp2(before - m)
-                    m_run[...] = m
-                    l_run[...] = fade * l_run[...] + lane_sums(p)
-                    acc[...] = fade * acc[...] + jnp.dot(p.astype(bf16), vals, preferred_element_type=f32)
-
-                o = acc[...] / jnp.sum(l_run[...], axis=1, keepdims=True)
+                    m_run[sub] = m
+                    l_run[sub] = fade * l_run[sub] + lane_sums(p)
+                    acc[sub] = fade * acc[sub] + jnp.dot(p.astype(bf16), vals, preferred_element_type=f32)
+
+            for sub in range(2):
+                o = acc[sub] / jnp.sum(l_run[sub], axis=1, keepdims=True)
                 o_st[rr, pl.ds(late * half_units + sub * sub_units, sub_units)] = o.astype(bf16).reshape(sub_units, half_rows, LANES)
 
         for t in range(tp_devs // 2):
@@ -479,16 +564,23 @@
                 wo_onward(o, h).start()
                 wo_handed(o, h).start()
 
-        @pl.when(piece == 2)
+        @pl.when(piece == 1)
         def _():
             for o, h in ((3, 1), (1, 0)):
                 wo_from(o, h).wait_recv()
                 wo_handed(o, h).start()
 
-    with jax.named_scope('a_wo2'):
-        for h in range(n_half):
-            wo_from(2, h).wait_recv()
-            wo_handed(2, h).start()
+        @pl.when(piece == 2)
+        def _():
+            for h in range(n_half):
+                t = column(2)
+                remote(wo_part(t, h), wo_part(t, h), wos_sem.at[h], wor_sem.at[h], sibling).wait_recv()
+                wo_handed(2, h).start()
+
+    remote(all_along, all_along, us_sem, ur_sem, sibling).wait_recv()
+    for o in range(1, x_devs):
+        wo_rest_handed(o).start()
+
     with jax.named_scope('a_owait'):
         pltpu.make_async_copy(og, og, or_sem).wait()
     for n in range(og.shape[0]):
@@ -497,6 +589,7 @@
         for o in range(x_devs):
             for h in range(n_half):
                 wo_handed(o, h, 1).wait_recv()
+            wo_rest_handed(o, 1).wait_recv()
 
     sub = hidden // LANES
     step = 2 * LANES
@@ -521,13 +614,20 @@
             direct(d, h).wait_send()
         for o in range(x_devs):
             for h in range(n_half):
-                handed(o, h).wait_send()
+                if o != 2:
+                    handed(o, h).wait_send()
                 wo_handed(o, h).wait_send()
+            wo_rest_handed(o).wait_send()
         for d, h in SEND_ORDER:
             wo_direct(d, h).wait_send()
+        for d in range(1, x_devs):
+            wo_across(d).wait_send()
+        remote(all_along, all_along, us_sem, ur_sem, sibling).wait_send()
         for o, h in ONWARD:
-            onward(h).wait_send()
             wo_onward(o, h).wait_send()
+            for part in range(2):
+                onward(h, part).wait_send()
+                handed_last(h, part).wait_send()
         for i in range(n_heads_loc):
             @pl.when(core * n_heads_loc + i != row)
             def _():
@@ -547,7 +647,7 @@
             remote(og, og, os_sem, or_sem, sibling).wait_send()
 
 
-def attention_residual(hidden_in, w_query, w_key, w_value, w_out, cp_devs, tp_devs):
+def attention_residual(hidden_in, w_query, w_key, w_value, w_out, expert_idx, local_exp, cp_devs, tp_devs, chunks):
     tok_dev, hidden = hidden_in.shape
     heads_loc, head_dim = w_query.shape[1:]
     if w_key.shape != w_query.shape or head_dim != LANES or tp_devs != RING * CORES or heads_loc * CORES != cp_devs:
@@ -562,16 +662,20 @@
     sub_rows = units // 4 * half_rows
     bf16, f32 = jnp.bfloat16, jnp.float32
     dma = pltpu.SemaphoreType.DMA
-    flat = [w.reshape(hidden, heads_loc * head_dim) for w in (w_query, w_key, w_value)]
+    n_dev = cp_devs * tp_devs
     return pl.pallas_call(
-        functools.partial(attention_kernel, cp_devs, tp_devs),
-        out_shape=jax.ShapeDtypeStruct((tok_dev, sub, LANES), bf16),
-        in_specs=[pl.BlockSpec(memory_space=pltpu.VMEM)] + [pl.BlockSpec(memory_space=pl.ANY)] * 4,
-        out_specs=pl.BlockSpec(memory_space=pltpu.VMEM),
+        functools.partial(attention_kernel, cp_devs, tp_devs, local_exp, chunks),
+        out_shape=[jax.ShapeDtypeStruct((tok_dev, sub, LANES), bf16), jax.ShapeDtypeStruct((n_dev, LANES), jnp.int32),
+                   jax.ShapeDtypeStruct(expert_idx.shape[::-1], jnp.int32)],
+        in_specs=[pl.BlockSpec(memory_space=pltpu.VMEM)] + [pl.BlockSpec(memory_space=pl.ANY)] * 4 + [pl.BlockSpec(memory_space=pltpu.VMEM)],
+        out_specs=[pl.BlockSpec(memory_space=pltpu.VMEM)] * 3,
         scratch_shapes=[
+            pltpu.VMEM((3, hidden, heads_loc, head_dim), bf16),
             pltpu.VMEM((3, hidden, heads_loc * head_dim), bf16),
-            pltpu.VMEM((batches, batch_units, half_rows, hidden), bf16),
-            pltpu.VMEM((batches, heads_loc, batch_units, 3, half_rows, LANES), bf16),
+            pltpu.VMEM((batches - 1, batch_units, half_rows, hidden), bf16),
+            pltpu.VMEM((2, batch_units, half_rows // 2, hidden), bf16),
+            pltpu.VMEM((batches - 1, heads_loc, batch_units, 3, half_rows, LANES), bf16),
+            pltpu.VMEM((2, heads_loc, batch_units, 3, half_rows // 2, LANES), bf16),
             pltpu.VMEM((half_cp, units, half_rows, LANES), bf16),
             pltpu.VMEM((cp_devs, units, 2, half_rows, LANES), bf16),
             pltpu.VMEM((half_cp, units, half_rows, LANES), bf16),
@@ -579,17 +683,19 @@
             pltpu.VMEM((tok_dev, hidden), bf16),
             pltpu.VMEM((n_heads * head_dim, hidden), bf16),
             pltpu.VMEM((tok_dev * sub, LANES), f32),
-            pltpu.VMEM((sub_rows, LANES), f32),
-            pltpu.VMEM((sub_rows, LANES), f32),
-            pltpu.VMEM((sub_rows, LANES), f32),
+            pltpu.VMEM((2, sub_rows, LANES), f32),
+            pltpu.VMEM((2, sub_rows, LANES), f32),
+            pltpu.VMEM((2, sub_rows, LANES), f32),
             dma((RING - 1, n_half)), dma((RING - 1, n_half)), dma((RING, n_half)), dma((RING, n_half)),
-            dma((2, heads_loc)), dma((half_cp, batches)), dma((half_cp, batches)), dma, dma((half_cp, batches)),
-            dma((RING - 1, n_half)), dma((RING - 1, n_half)), dma((RING, n_half)), dma((RING, n_half)), dma, dma, dma((4,)),
+            dma((2, 2)), dma((2, 2)), dma((2, 2)), dma((2, 2)),
+            dma((2, heads_loc)), dma((half_cp, len(STEPS))), dma((half_cp, len(STEPS))), dma, dma((half_cp, len(STEPS))),
+            dma((RING - 1, n_half)), dma((RING - 1, n_half)), dma((RING, n_half)), dma((RING, n_half)), dma((2,)), dma((2,)),
+            dma((RING - 1,)), dma((RING - 1,)), dma, dma, dma((RING,)), dma((RING,)), dma, dma, dma((4,)),
         ],
         compiler_params=pltpu.CompilerParams(collective_id=1, has_side_effects=True, vmem_limit_bytes=67043328),
         cost_estimate=pl.CostEstimate(flops=12 * 10 ** 9, bytes_accessed=16 * 10 ** 6, transcendentals=10 ** 7),
         name='attention_exchange',
-    )(hidden_in.reshape(n_half, half_rows, hidden), *flat, w_out.reshape(heads_loc * head_dim, hidden))
+    )(hidden_in.reshape(n_half, half_rows, hidden), w_query, w_key, w_value, w_out.reshape(heads_loc * head_dim, hidden), expert_idx.T)
 
 
 from jax.sharding import PartitionSpec as P
@@ -602,7 +708,8 @@
     expert_spec = P(('cp', 'tp'), None, None)
 
     def device_step(hidden_in, w_query, w_key, w_value, w_out, expert_idx, gate_vals, w_gate, w_up, w_down):
-        h_tiles = attention_residual(hidden_in, w_query, w_key, w_value, w_out, cp_devs, tp_devs)
-        return moe(h_tiles, expert_idx, gate_vals, w_gate, w_up, w_down, cp_devs, tp_devs)
+        chunks = 3
+        h_tiles, src, pos = attention_residual(hidden_in, w_query, w_key, w_value, w_out, expert_idx, w_gate.shape[0], cp_devs, tp_devs, chunks)
+        return moe(h_tiles, src, pos, gate_vals, w_gate, w_up, w_down, cp_devs, tp_devs, chunks)
 
     return jax.shard_map(device_step, mesh=mesh, in_specs=(row_spec, head_spec, head_spec, head_spec, P('tp', None, None), row_spec, row_spec, expert_spec, expert_spec, expert_spec), out_specs=row_spec, check_vma=False)

time: 200 us -> 181 us (0.905)
  Pallas kernels: 188 us -> 179 us
  local copies, waits for them, and re-layouts: 7.67 us -> 2.09 us
  other arithmetic: 3.09 us -> 0 us
    pallas_call x1, Pallas kernels: 89.8 us -> 80.1 us  [attention_residual(): pl.pallas_call(functools.partial(attention_kernel, cp_devs, tp_devs, loca...]
    reshape x1 -> x0, local copies, waits for them, and re-layouts: 3.23 us -> none  [attention_residual(): w.reshape(hidden, heads_loc * head_dim)]
    unnamed x2 -> x1, local copies, waits for them, and re-layouts: 4.44 us -> 2.09 us
where the time goes in v3:
time: 181 us
  Pallas kernels  179 us (99%)
  local copies, waits for them, and re-layouts  2.09 us (1%)
    pallas_call x1, Pallas kernels, moe(): pl.pallas_call(functools.partial(moe_kernel, cp_devs, tp_devs, chunks), o...  98.8 us
    pallas_call x1, Pallas kernels, attention_residual(): pl.pallas_call(functools.partial(attention_kernel, cp_devs, tp_devs, loca...  80.1 us

profile of v3, /device:TPU:97, one launch (start us, length us, event | category | flops | bytes accessed | tf_op | source)
XLA Modules:
  0.0 181.0 jit_solution(17147708667089869181)
XLA Ops:
  0.0 80.1 %attention_exchange.1 = (bf16[192,16,128]{2,1,0:T(8,128)(2,1)}, s32[32,128]{1,0:T(8,128)}, s32[6,192]{1,0:T(8,128)}) custom-call(bf16[2,96,2048]{2,1,0:T(8,128)(2,1)} %bitcast.5, bf16[2048,2,128]{2,1,0:T(2,128)(2,1)} %wq_ref.1, bf16[2048,2,128]{2,1,0:T(2,128)(2,1)} %wk_ref.1, bf16[2048,2,128]{2,1,0:T(2,128)(2,1)} %wv_ref.1, bf16[256,2048]{1,0:T(8,128)(2,1)} %bitcast.4, ...), custom_call_target="tpu_custom_call" | custom-call | flops 12000000000 | bytes 16000000 | tf_op jit(solution)/shard_map/attention_exchange/pallas_call | solution.py:666
  80.1 98.8 %moe_exchange.1 = bf16[192,2048]{1,0:T(8,128)(2,1)} custom-call(s32[32,128]{1,0:T(8,128)} %get-tuple-element.8.src_ref, s32[6,192]{1,0:T(8,128)} %get-tuple-element.9.pos_ref, f32[6,192]{1,0:T(8,128)} %bitcast.7, bf16[192,16,128]{2,1,0:T(8,128)(2,1)} %get-tuple-element.10.h_ref, bf16[2,2048,1408]{2,1,0:T(8,128)(2,1)} %wg_ref.1, ...), custom_call_target="tpu_custom_call" | custom-call | flops 19931332608 | bytes 34603008 | tf_op jit(solution)/shard_map/moe_exchange/pallas_call | solution.py:219
  178.9 2.1 %copy.12 = bf16[192,2048]{1,0:T(8,128)(2,1)} copy(bf16[192,2048]{1,0:T(8,128)(2,1)} %moe_exchange.1) | data formatting | bytes 1572864

commit v4 on v3

--- a/solution.py
+++ b/solution.py
@@ -56,16 +56,6 @@
 
     def dn_copy(e, j):
         return pltpu.make_async_copy(wd_ref.at[e, :, pl.ds(pl.multiple_of(j * dn_cols, dn_cols), dn_cols)], wdv.at[e, j], w_sem.at[1, e])
-
-    for e in range(local_exp):
-        @pl.loop(0, gu_tiles)
-        def _(j):
-            gu_copy(e, j, 0, wg_ref).start()
-            gu_copy(e, j, 1, wu_ref).start()
-
-        @pl.loop(0, dn_tiles)
-        def _(j):
-            dn_copy(e, j).start()
 
     def fill(dev, carry):
         for c in range(chunks):
@@ -104,6 +94,16 @@
         with jax.named_scope('m_dstart'):
             all_of(dispatch, c, 'start')
         pltpu.make_async_copy(send.at[c, me], recv.at[c, me], loc_sem.at[c]).start()
+
+    for e in range(local_exp):
+        @pl.loop(0, gu_tiles)
+        def _(j):
+            gu_copy(e, j, 0, wg_ref).start()
+            gu_copy(e, j, 1, wu_ref).start()
+
+        @pl.loop(0, dn_tiles)
+        def _(j):
+            dn_copy(e, j).start()
 
     for c in range(chunks):
         pltpu.make_async_copy(send.at[c, me], recv.at[c, me], loc_sem.at[c]).wait()
@@ -250,14 +250,22 @@
            ((3, 0, 0), (3, 1, 0), (1, 0, 1), (1, 1, 1)),
            ((3, 0, 1), (3, 1, 1), (1, 0, 0), (1, 1, 0)),
            ((2, 0, 0), (2, 0, 1), (2, 1, 0), (2, 1, 1)))
-STEPS = ((0, 0, 1), (1, 0, 1), (2, 0, 1), (3, 0, 2), (3, 1, 2))
+STEPS = ((0, 0, 1), (1, 0, 2), (1, 1, 2), (2, 0, 2), (2, 1, 2), (3, 0, 2), (3, 1, 2))
 SEND_ORDER = ((1, 0), (3, 1), (1, 1), (3, 0))
 ONWARD = {(3, 0): 1, (1, 1): 3}
+ORDERS = ((0, 1, 2, 3), (2, 3, 0, 1), (0, 3, 1, 2), (2, 1, 3, 0))
+
+
+def pick(values, at):
+    out = values[-1]
+    for n in range(len(values) - 1):
+        out = jnp.where(at == n, values[n], out)
+    return out
 
 
 def attention_kernel(cp_devs, tp_devs, local_exp, chunks, hid_ref, wq_ref, wk_ref, wv_ref, wo_ref, idx_ref, h_ref, src_ref, pos_ref,
-                     w_raw, w_in, xg, x_last, stage, stage_last, q_all, kv_all, o_st, og, o_rows, wo_all, wide, acc, m_run, l_run,
-                     xs_sem, xr_sem, fs_sem, fr_sem, ons_sem, onr_sem, fls_sem, flr_sem, ys_sem, yq_sem, ykv_sem, ks_sem, kr_sem, ws_sem, wr_sem, wfs_sem, wfr_sem, wos_sem, wor_sem, vs_sem, vr_sem, us_sem, ur_sem, hs_sem, hr_sem, os_sem, or_sem, in_sem):
+                     w_raw, w_in, xg, x_part, stage, stage_part, q_all, kv_all, o_st, og, o_rows, wo_all, wide, acc, m_run, l_run,
+                     xs_sem, xr_sem, fs_sem, fr_sem, ons_sem, onr_sem, ys_sem, yq_sem, ykv_sem, ks_sem, kr_sem, ws_sem, wr_sem, wfs_sem, wfr_sem, wos_sem, wor_sem, vs_sem, vr_sem, us_sem, ur_sem, hs_sem, hr_sem, os_sem, or_sem, in_sem):
     row, tp = lax.axis_index('cp'), lax.axis_index('tp')
     col, core = tp // CORES, lax.rem(tp, CORES)
     x_devs = tp_devs // CORES
@@ -267,7 +275,7 @@
     half_units = units // 2
     half_cp = cp_devs // 2
     batch_units = len(BATCHES[0])
-    n_heads_loc = stage.shape[1]
+    n_heads_loc = stage.shape[0]
     wo_rows = wo_ref.shape[0]
     f32, bf16 = jnp.float32, jnp.bfloat16
     mesh_id = pl.DeviceIdType.MESH
@@ -291,39 +299,38 @@
     loads.append(pltpu.make_async_copy(wo_ref, wo_all.at[pl.ds(pl.multiple_of(tp * wo_rows, wo_rows), wo_rows)], in_sem.at[3]))
     for load in loads:
         load.start()
-    xg[0, 0] = hid_ref[0]
-    xg[0, 1] = hid_ref[1]
+    xg[0] = hid_ref[0]
+    xg[1] = hid_ref[1]
     with jax.named_scope('a_barrier'):
         pl.semaphore_wait(barrier, n_dev - 1)
 
     where = {och: (b, u) for b, batch in enumerate(BATCHES) for u, och in enumerate(batch)}
 
-    def direct(d, h):
+    part_rows = x_part.shape[3]
+
+    def landing(o, c, h, part):
+        b, u = where[(o, c, h)]
+        return x_part.at[b - 1, part, u]
+
+    def direct(d, h, part):
         o = x_devs - d
-        b, u = where[(o, 0, h)]
-        return remote(hid_ref.at[h], xg.at[b, u], xs_sem.at[d - 1, h], xr_sem.at[o - 1, h], beside(d))
-
-    last_rows = x_last.shape[2]
+        return remote(hid_ref.at[h, pl.ds(part * part_rows, part_rows)], landing(o, 0, h, part), xs_sem.at[d - 1, h, part], xr_sem.at[o - 1, h, part], beside(d))
 
     def onward(h, part):
         o = 3 if h == 0 else 1
-        b, u = where[(o, 0, h)]
-        return remote(xg.at[b, u, pl.ds(part * last_rows, last_rows)], x_last.at[part, where[(2, 0, h)][1]], ons_sem.at[h, part], onr_sem.at[h, part],
-                      beside(ONWARD[(o, h)]))
-
-    def handed_last(h, part):
-        return remote(x_last.at[part, where[(2, 0, h)][1]], x_last.at[part, where[(2, 1, h)][1]], fls_sem.at[h, part], flr_sem.at[h, part], sibling)
-
-    def handed(o, h):
-        b, u = where[(o, 0, h)]
-        b2, u2 = where[(o, 1, h)]
-        src = hid_ref.at[h] if o == 0 else xg.at[b, u]
-        return remote(src, xg.at[b2, u2], fs_sem.at[o, h], fr_sem.at[o, h], sibling)
+        return remote(landing(o, 0, h, part), landing(2, 0, h, part), ons_sem.at[h, part], onr_sem.at[h, part], beside(ONWARD[(o, h)]))
+
+    def handed(o, h, part):
+        return remote(landing(o, 0, h, part), landing(o, 1, h, part), fs_sem.at[o, h, part], fr_sem.at[o, h, part], sibling)
+
+    def handed_own(h):
+        return remote(hid_ref.at[h], xg.at[where[(0, 1, h)][1]], fs_sem.at[0, h, 0], fr_sem.at[0, h, 0], sibling)
 
     for h in range(n_half):
-        handed(0, h).start()
+        handed_own(h).start()
     for d, h in SEND_ORDER:
-        direct(d, h).start()
+        for part in range(2):
+            direct(d, h, part).start()
 
     def unit_of(o, c, h):
         return (lax.rem(col + o, x_devs) * CORES + lax.rem(core + c, CORES)) * n_half + h
@@ -335,7 +342,7 @@
     def exchange(step):
         b, part, parts = STEPS[step]
         batch, some = rows_of(step)
-        done = stage.at[b] if parts == 1 else stage_last.at[part]
+        done = stage if parts == 1 else stage_part.at[b - 1, part]
         for i in range(n_heads_loc):
             to_row = core * n_heads_loc + i
             own = to_row == row
@@ -405,8 +412,7 @@
         return remote(part, part, hs_sem.at[o], hr_sem.at[o], sibling)
 
     def wo_start():
-        for d in range(1, x_devs):
-            wo_across(d).start()
+        wo_across(2).start()
         for d, h in SEND_ORDER:
             wo_direct(d, h).start()
         for h in range(n_half):
@@ -438,42 +444,44 @@
         with jax.named_scope('a_xwait'):
             for o, c, h in BATCHES[b]:
                 if c == 0 and o:
-                    (onward(h, part) if o == 2 else direct(x_devs - o, h)).wait_recv()
+                    (onward(h, part) if o == 2 else direct(x_devs - o, h, part)).wait_recv()
                     if (o, h) in ONWARD:
-                        onward(h, 0).start()
-                        onward(h, 1).start()
-                    (handed_last(h, part) if o == 2 else handed(o, h)).start()
+                        onward(h, part).start()
+                    handed(o, h, part).start()
             for o, c, h in BATCHES[b]:
                 if c == 1:
-                    (handed_last(h, part) if o == 2 else handed(o, h)).wait_recv()
-
+                    (handed(o, h, part) if o else handed_own(h)).wait_recv()
+
+        if step == len(STEPS) - 2:
+            wo_across(1).start()
+            wo_across(3).start()
+        if step == len(STEPS) - 1:
+            wo_start()
         with jax.named_scope('a_qkv'):
             n_rows = half_rows // parts
 
             @pl.loop(0, 3)
             def _(n):
-                x = xg[b] if parts == 1 else x_last[part]
+                x = xg[...] if parts == 1 else x_part[b - 1, part]
                 y = jnp.dot(x.reshape(batch_units * n_rows, hidden), w_in[n], preferred_element_type=f32).astype(bf16)
                 for i in range(n_heads_loc):
                     for u in range(batch_units):
                         val = y[u * n_rows:(u + 1) * n_rows, i * LANES:(i + 1) * LANES]
                         if parts == 1:
-                            stage[b, i, u, n] = val
+                            stage[i, u, n] = val
                         else:
-                            stage_last[part, i, u, n] = val
+                            stage_part[b - 1, part, i, u, n] = val
 
         with jax.named_scope('a_exch'):
             exchange(step)
-            if step == 1:
-                wo_start()
         with jax.named_scope('a_share'):
-            if step in (1, 2):
-                share(step - 1)
+            if step >= 2:
+                share(step - 2)
         if step == 0:
             with jax.named_scope('a_tables'):
                 routing_tables(idx_ref, src_ref, pos_ref, n_dev, local_exp, chunks)
     with jax.named_scope('a_share_last'):
-        for step in range(2, len(STEPS)):
+        for step in range(len(STEPS) - 2, len(STEPS)):
             share(step)
     with jax.named_scope('a_wospread'):
         wo_spread()
@@ -503,7 +511,9 @@
         return total
 
     @pl.loop(0, 2 * half_cp)
-    def _(piece):
+    def _(turn):
+        diagonal = lax.rem(row + col, len(ORDERS))
+        piece = pick([pick([order[t] for order in ORDERS], diagonal) for t in range(len(ORDERS))], turn)
         rr, late = piece // 2, lax.rem(piece, 2)
         block = core * half_cp + rr
         place = jnp.where(late == 0, block, 2 * cp_devs - 1 - block)
@@ -557,26 +567,23 @@
             def _():
                 remote(src, og.at[head], os_sem, or_sem, {'cp': block, 'tp': to_tp}).start()
 
-        @pl.when(piece == 0)
+        @pl.when(turn == 1)
         def _():
             for o, h in ONWARD:
                 wo_from(o, h).wait_recv()
                 wo_onward(o, h).start()
                 wo_handed(o, h).start()
 
-        @pl.when(piece == 1)
+        @pl.when(turn == 2)
         def _():
             for o, h in ((3, 1), (1, 0)):
                 wo_from(o, h).wait_recv()
                 wo_handed(o, h).start()
 
-        @pl.when(piece == 2)
-        def _():
-            for h in range(n_half):
-                t = column(2)
-                remote(wo_part(t, h), wo_part(t, h), wos_sem.at[h], wor_sem.at[h], sibling).wait_recv()
-                wo_handed(2, h).start()
-
+    for h in range(n_half):
+        t = column(2)
+        remote(wo_part(t, h), wo_part(t, h), wos_sem.at[h], wor_sem.at[h], sibling).wait_recv()
+        wo_handed(2, h).start()
     remote(all_along, all_along, us_sem, ur_sem, sibling).wait_recv()
     for o in range(1, x_devs):
         wo_rest_handed(o).start()
@@ -611,11 +618,15 @@
 
     with jax.named_scope('a_drain'):
         for d, h in SEND_ORDER:
-            direct(d, h).wait_send()
+            for part in range(2):
+                direct(d, h, part).wait_send()
         for o in range(x_devs):
             for h in range(n_half):
-                if o != 2:
-                    handed(o, h).wait_send()
+                if o:
+                    for part in range(2):
+                        handed(o, h, part).wait_send()
+                else:
+                    handed_own(h).wait_send()
                 wo_handed(o, h).wait_send()
             wo_rest_handed(o).wait_send()
         for d, h in SEND_ORDER:
@@ -627,7 +638,6 @@
             wo_onward(o, h).wait_send()
             for part in range(2):
                 onward(h, part).wait_send()
-                handed_last(h, part).wait_send()
         for i in range(n_heads_loc):
             @pl.when(core * n_heads_loc + i != row)
             def _():
@@ -672,10 +682,10 @@
         scratch_shapes=[
             pltpu.VMEM((3, hidden, heads_loc, head_dim), bf16),
             pltpu.VMEM((3, hidden, heads_loc * head_dim), bf16),
-            pltpu.VMEM((batches - 1, batch_units, half_rows, hidden), bf16),
-            pltpu.VMEM((2, batch_units, half_rows // 2, hidden), bf16),
-            pltpu.VMEM((batches - 1, heads_loc, batch_units, 3, half_rows, LANES), bf16),
-            pltpu.VMEM((2, heads_loc, batch_units, 3, half_rows // 2, LANES), bf16),
+            pltpu.VMEM((batch_units, half_rows, hidden), bf16),
+            pltpu.VMEM((batches - 1, 2, batch_units, half_rows // 2, hidden), bf16),
+            pltpu.VMEM((heads_loc, batch_units, 3, half_rows, LANES), bf16),
+            pltpu.VMEM((batches - 1, 2, heads_loc, batch_units, 3, half_rows // 2, LANES), bf16),
             pltpu.VMEM((half_cp, units, half_rows, LANES), bf16),
             pltpu.VMEM((cp_devs, units, 2, half_rows, LANES), bf16),
             pltpu.VMEM((half_cp, units, half_rows, LANES), bf16),
@@ -686,8 +696,8 @@
             pltpu.VMEM((2, sub_rows, LANES), f32),
             pltpu.VMEM((2, sub_rows, LANES), f32),
             pltpu.VMEM((2, sub_rows, LANES), f32),
-            dma((RING - 1, n_half)), dma((RING - 1, n_half)), dma((RING, n_half)), dma((RING, n_half)),
-            dma((2, 2)), dma((2, 2)), dma((2, 2)), dma((2, 2)),
+            dma((RING - 1, n_half, 2)), dma((RING - 1, n_half, 2)), dma((RING, n_half, 2)), dma((RING, n_half, 2)),
+            dma((n_half, 2)), dma((n_half, 2)),
             dma((2, heads_loc)), dma((half_cp, len(STEPS))), dma((half_cp, len(STEPS))), dma, dma((half_cp, len(STEPS))),
             dma((RING - 1, n_half)), dma((RING - 1, n_half)), dma((RING, n_half)), dma((RING, n_half)), dma((2,)), dma((2,)),
             dma((RING - 1,)), dma((RING - 1,)), dma, dma, dma((RING,)), dma((RING,)), dma, dma, dma((4,)),

time: 181 us -> 181 us (level)
  no operation moved by 1% of the time
where the time goes in v4:
time: 181 us
  Pallas kernels  179 us (99%)
  local copies, waits for them, and re-layouts  2.09 us (1%)
    pallas_call x1, Pallas kernels, moe(): pl.pallas_call(functools.partial(moe_kernel, cp_devs, tp_devs, chunks), o...  99.6 us
    pallas_call x1, Pallas kernels, attention_residual(): pl.pallas_call(functools.partial(attention_kernel, cp_devs, tp_devs, loca...  79.4 us

profile of v4, /device:TPU:97, one launch (start us, length us, event | category | flops | bytes accessed | tf_op | source)
XLA Modules:
  0.0 181.1 jit_solution(14839905979053041502)
XLA Ops:
  0.0 79.4 %attention_exchange.1 = (bf16[192,16,128]{2,1,0:T(8,128)(2,1)}, s32[32,128]{1,0:T(8,128)}, s32[6,192]{1,0:T(8,128)}) custom-call(bf16[2,96,2048]{2,1,0:T(8,128)(2,1)} %bitcast.5, bf16[2048,2,128]{2,1,0:T(2,128)(2,1)} %wq_ref.1, bf16[2048,2,128]{2,1,0:T(2,128)(2,1)} %wk_ref.1, bf16[2048,2,128]{2,1,0:T(2,128)(2,1)} %wv_ref.1, bf16[256,2048]{1,0:T(8,128)(2,1)} %bitcast.4, ...), custom_call_target="tpu_custom_call" | custom-call | flops 12000000000 | bytes 16000000 | tf_op jit(solution)/shard_map/attention_exchange/pallas_call | solution.py:676
  79.4 99.6 %moe_exchange.1 = bf16[192,2048]{1,0:T(8,128)(2,1)} custom-call(s32[32,128]{1,0:T(8,128)} %get-tuple-element.8.src_ref, s32[6,192]{1,0:T(8,128)} %get-tuple-element.9.pos_ref, f32[6,192]{1,0:T(8,128)} %bitcast.7, bf16[192,16,128]{2,1,0:T(8,128)(2,1)} %get-tuple-element.10.h_ref, bf16[2,2048,1408]{2,1,0:T(8,128)(2,1)} %wg_ref.1, ...), custom_call_target="tpu_custom_call" | custom-call | flops 19931332608 | bytes 34603008 | tf_op jit(solution)/shard_map/moe_exchange/pallas_call | solution.py:219
  179.0 2.1 %copy.12 = bf16[192,2048]{1,0:T(8,128)(2,1)} copy(bf16[192,2048]{1,0:T(8,128)(2,1)} %moe_exchange.1) | data formatting | bytes 1572864

commit v5 on v4

--- a/solution.py
+++ b/solution.py
@@ -56,6 +56,16 @@
 
     def dn_copy(e, j):
         return pltpu.make_async_copy(wd_ref.at[e, :, pl.ds(pl.multiple_of(j * dn_cols, dn_cols), dn_cols)], wdv.at[e, j], w_sem.at[1, e])
+
+    for e in range(local_exp):
+        @pl.loop(0, gu_tiles)
+        def _(j):
+            gu_copy(e, j, 0, wg_ref).start()
+            gu_copy(e, j, 1, wu_ref).start()
+
+        @pl.loop(0, dn_tiles)
+        def _(j):
+            dn_copy(e, j).start()
 
     def fill(dev, carry):
         for c in range(chunks):
@@ -94,16 +104,6 @@
         with jax.named_scope('m_dstart'):
             all_of(dispatch, c, 'start')
         pltpu.make_async_copy(send.at[c, me], recv.at[c, me], loc_sem.at[c]).start()
-
-    for e in range(local_exp):
-        @pl.loop(0, gu_tiles)
-        def _(j):
-            gu_copy(e, j, 0, wg_ref).start()
-            gu_copy(e, j, 1, wu_ref).start()
-
-        @pl.loop(0, dn_tiles)
-        def _(j):
-            dn_copy(e, j).start()
 
     for c in range(chunks):
         pltpu.make_async_copy(send.at[c, me], recv.at[c, me], loc_sem.at[c]).wait()
@@ -599,7 +599,7 @@
             wo_rest_handed(o, 1).wait_recv()
 
     sub = hidden // LANES
-    step = 2 * LANES
+    step = 4 * LANES
     rows = n_half * half_rows
 
     with jax.named_scope('a_proj'):

time: 181 us -> 177 us (0.978)
  Pallas kernels: 179 us -> 175 us
    pallas_call x1, Pallas kernels: 99.6 us -> 96.1 us  [moe(): pl.pallas_call(functools.partial(moe_kernel, cp_devs, tp_devs, chunks), o...]
where the time goes in v5:
time: 177 us
  Pallas kernels  175 us (99%)
  local copies, waits for them, and re-layouts  2.09 us (1%)
    pallas_call x1, Pallas kernels, moe(): pl.pallas_call(functools.partial(moe_kernel, cp_devs, tp_devs, chunks), o...  96.1 us
    pallas_call x1, Pallas kernels, attention_residual(): pl.pallas_call(functools.partial(attention_kernel, cp_devs, tp_devs, loca...  78.6 us

profile of v5, /device:TPU:97, one launch (start us, length us, event | category | flops | bytes accessed | tf_op | source)
XLA Modules:
  0.0 176.7 jit_solution(9456495755269205557)
XLA Ops:
  0.0 78.6 %attention_exchange.1 = (bf16[192,16,128]{2,1,0:T(8,128)(2,1)}, s32[32,128]{1,0:T(8,128)}, s32[6,192]{1,0:T(8,128)}) custom-call(bf16[2,96,2048]{2,1,0:T(8,128)(2,1)} %bitcast.5, bf16[2048,2,128]{2,1,0:T(2,128)(2,1)} %wq_ref.1, bf16[2048,2,128]{2,1,0:T(2,128)(2,1)} %wk_ref.1, bf16[2048,2,128]{2,1,0:T(2,128)(2,1)} %wv_ref.1, bf16[256,2048]{1,0:T(8,128)(2,1)} %bitcast.4, ...), custom_call_target="tpu_custom_call" | custom-call | flops 12000000000 | bytes 16000000 | tf_op jit(solution)/shard_map/attention_exchange/pallas_call | solution.py:676
  78.6 96.1 %moe_exchange.1 = bf16[192,2048]{1,0:T(8,128)(2,1)} custom-call(s32[32,128]{1,0:T(8,128)} %get-tuple-element.8.src_ref, s32[6,192]{1,0:T(8,128)} %get-tuple-element.9.pos_ref, f32[6,192]{1,0:T(8,128)} %bitcast.7, bf16[192,16,128]{2,1,0:T(8,128)(2,1)} %get-tuple-element.10.h_ref, bf16[2,2048,1408]{2,1,0:T(8,128)(2,1)} %wg_ref.1, ...), custom_call_target="tpu_custom_call" | custom-call | flops 19931332608 | bytes 34603008 | tf_op jit(solution)/shard_map/moe_exchange/pallas_call | solution.py:219
  174.7 2.1 %copy.12 = bf16[192,2048]{1,0:T(8,128)(2,1)} copy(bf16[192,2048]{1,0:T(8,128)(2,1)} %moe_exchange.1) | data formatting | bytes 1572864
